TPU v7x, 32 devices: a whole 2x2x4 slice. The times are simulated.
32 devices in a mesh: dp: 32 (over z, y, x, core).
Axes of the slice: x: 2, y: 2, z: 4, core: 2. Of those that a mesh axis runs over, the one named last changes fastest.
Arguments:
- x_in: bfloat16 [512, 192, 2048], P('dp')
- grad_y: bfloat16 [512, 192, 2048], P('dp')
- g_in: bfloat16 [2048], replicated
- w_q: bfloat16 [2048, 16, 192], replicated
- w_dkv: bfloat16 [2048, 512], replicated
- g_kv: bfloat16 [512], replicated
- w_kr: bfloat16 [2048, 64], replicated
- w_uk: bfloat16 [512, 16, 128], replicated
- w_uv: bfloat16 [512, 16, 128], replicated
- w_o: bfloat16 [16, 128, 2048], replicated
Outputs:
- output 1: bfloat16 [512, 192, 2048], P('dp')
- output 2: float32 [2048], P('dp')
- output 3: float32 [6291456], P('dp')
- output 4: float32 [1048576], P('dp')
- output 5: float32 [512], P('dp')
- output 6: float32 [131072], P('dp')
- output 7: float32 [1048576], P('dp')
- output 8: float32 [1048576], P('dp')
- output 9: float32 [4194304], P('dp')
All inputs are finite; a program needn't handle non-finite values.
Results may differ from a plain program's by a relative error of at most 0.0100842.
Values sent between devices are 32-bit elements.
A program may use at most 1 GiB of HBM per device.

v0:
```python
import jax
import jax.numpy as jnp
from jax import lax
from jax.sharding import PartitionSpec as P

EPS = 1e-6
ROPE_BASE = 10000.0


def rope_tables(seq_len, rot_dim):
    half_dim = rot_dim // 2
    inv_freq = jnp.power(ROPE_BASE, -2.0 * jnp.arange(half_dim, dtype=jnp.float32) / rot_dim)
    angles = jnp.arange(seq_len, dtype=jnp.float32)[:, None] * inv_freq[None, :]
    return jnp.cos(angles), jnp.sin(angles)


def apply_rope(vals, cos_t, sin_t):
    half_dim = vals.shape[-1] // 2
    first = vals[..., :half_dim]
    second = vals[..., half_dim:]
    return jnp.concatenate([first * cos_t - second * sin_t, second * cos_t + first * sin_t], axis=-1)


def rope_back(grads_in, cos_t, sin_t):
    half_dim = grads_in.shape[-1] // 2
    first = grads_in[..., :half_dim]
    second = grads_in[..., half_dim:]
    return jnp.concatenate([first * cos_t + second * sin_t, second * cos_t - first * sin_t], axis=-1)


def contract(eq_form, operand_a, operand_b):
    return jnp.einsum(eq_form, operand_a, operand_b, preferred_element_type=jnp.float32)


def block_grads(x_in, grad_y, g_in, w_q, w_dkv, g_kv, w_kr, w_uk, w_uv, w_o):
    seq_len = x_in.shape[1]
    nope_dim = w_uk.shape[2]
    qk_scale = w_q.shape[2] ** -0.5
    cos_t, sin_t = rope_tables(seq_len, w_kr.shape[1])
    cos_h = cos_t[:, None, :]
    sin_h = sin_t[:, None, :]
    x_wide = x_in.astype(jnp.float32)
    inv_x = lax.rsqrt(jnp.mean(x_wide * x_wide, axis=-1, keepdims=True) + EPS)
    x_hat = x_wide * inv_x
    gain_in = g_in.astype(jnp.float32)
    hidden = (x_hat * gain_in).astype(jnp.bfloat16)
    q_full = contract('bsd,dhk->bshk', hidden, w_q)
    q_nope = q_full[..., :nope_dim].astype(jnp.bfloat16)
    q_rot = apply_rope(q_full[..., nope_dim:], cos_h, sin_h).astype(jnp.bfloat16)
    latent = contract('bsd,dr->bsr', hidden, w_dkv)
    inv_lat = lax.rsqrt(jnp.mean(latent * latent, axis=-1, keepdims=True) + EPS)
    lat_hat = latent * inv_lat
    gain_kv = g_kv.astype(jnp.float32)
    lat_norm = (lat_hat * gain_kv).astype(jnp.bfloat16)
    k_rot = apply_rope(contract('bsd,de->bse', hidden, w_kr), cos_t, sin_t).astype(jnp.bfloat16)
    k_nope = contract('bsr,rhk->bshk', lat_norm, w_uk).astype(jnp.bfloat16)
    v_heads = contract('bsr,rhk->bshk', lat_norm, w_uv).astype(jnp.bfloat16)
    scores = (contract('bqhk,bthk->bhqt', q_nope, k_nope) + contract('bqhe,bte->bhqt', q_rot, k_rot)) * qk_scale
    positions = jnp.arange(seq_len)
    causal = positions[:, None] >= positions[None, :]
    attn_prob = jax.nn.softmax(jnp.where(causal, scores, -1e30), axis=-1)
    prob_low = attn_prob.astype(jnp.bfloat16)
    attn_out = contract('bhqt,bthk->bqhk', prob_low, v_heads).astype(jnp.bfloat16)
    d_w_o = contract('bshk,bsd->hkd', attn_out, grad_y)
    d_attn = contract('bsd,hkd->bshk', grad_y, w_o).astype(jnp.bfloat16)
    d_prob = contract('bqhk,bthk->bhqt', d_attn, v_heads)
    d_values = contract('bhqt,bqhk->bthk', prob_low, d_attn).astype(jnp.bfloat16)
    row_dot = jnp.sum(attn_prob * d_prob, axis=-1, keepdims=True)
    d_scores = (attn_prob * (d_prob - row_dot) * qk_scale).astype(jnp.bfloat16)
    d_q_nope = contract('bhqt,bthk->bqhk', d_scores, k_nope)
    d_q_rot = contract('bhqt,bte->bqhe', d_scores, k_rot)
    d_k_nope = contract('bhqt,bqhk->bthk', d_scores, q_nope).astype(jnp.bfloat16)
    d_k_rot = contract('bhqt,bqhe->bte', d_scores, q_rot)
    d_query = jnp.concatenate([d_q_nope, rope_back(d_q_rot, cos_h, sin_h)], axis=-1).astype(jnp.bfloat16)
    d_kr_in = rope_back(d_k_rot, cos_t, sin_t).astype(jnp.bfloat16)
    d_w_uv = contract('bsr,bshk->rhk', lat_norm, d_values)
    d_w_uk = contract('bsr,bshk->rhk', lat_norm, d_k_nope)
    d_w_kr = contract('bsd,bse->de', hidden, d_kr_in)
    d_lat = contract('bshk,rhk->bsr', d_k_nope, w_uk) + contract('bshk,rhk->bsr', d_values, w_uv)
    d_g_kv = jnp.sum(d_lat * lat_hat, axis=(0, 1))
    d_lat_hat = d_lat * gain_kv
    d_latent = (inv_lat * (d_lat_hat - lat_hat * jnp.mean(d_lat_hat * lat_hat, axis=-1, keepdims=True))).astype(jnp.bfloat16)
    d_w_q = contract('bsd,bshk->dhk', hidden, d_query)
    d_w_dkv = contract('bsd,bsr->dr', hidden, d_latent)
    d_hidden = (contract('bshk,dhk->bsd', d_query, w_q) + contract('bsr,dr->bsd', d_latent, w_dkv)
                + contract('bse,de->bsd', d_kr_in, w_kr))
    d_g_in = jnp.sum(d_hidden * x_hat, axis=(0, 1))
    d_x_hat = d_hidden * gain_in
    grad_x = (grad_y.astype(jnp.float32) + inv_x * (d_x_hat - x_hat * jnp.mean(d_x_hat * x_hat, axis=-1, keepdims=True))).astype(jnp.bfloat16)
    return grad_x, [d_g_in, d_w_q, d_w_dkv, d_g_kv, d_w_kr, d_w_uk, d_w_uv, d_w_o]


def solution(mesh):
    n_dev = mesh.shape['dp']

    def device_step(x_in, grad_y, g_in, w_q, w_dkv, g_kv, w_kr, w_uk, w_uv, w_o):
        grad_x, local_grads = block_grads(x_in, grad_y, g_in, w_q, w_dkv, g_kv, w_kr, w_uk, w_uv, w_o)
        grad_shards = [lax.psum_scatter(local_grad.reshape(-1), 'dp', scatter_dimension=0, tiled=True) / n_dev
                       for local_grad in local_grads]
        return tuple([grad_x] + grad_shards)

    batch_spec = P('dp')
    full_spec = P()
    return jax.shard_map(device_step, mesh=mesh,
                         in_specs=(batch_spec, batch_spec) + (full_spec,) * 8,
                         out_specs=(batch_spec,) * 9, check_vma=False)
```

profile of v0, /device:TPU:0, one launch (start us, length us, event | category | flops | bytes accessed | tf_op | source)
XLA Modules:
  0.0 1706.2 jit_solution(2012882182192620375)
XLA Ops:
  7.2 0.0 copy-start
  7.2 0.0 all-reduce.12.cloned.1.call-start
  7.3 0.6 iota_compare_fusion
  7.9 7.1 fusion.18
  15.1 0.8 fusion.110
  15.9 60.9 %fusion.38 = f32[16,192,16,192]{1,3,2,0:T(8,128)} fusion(bf16[2048,16,192]{0,2,1:T(8,128)(2,1)} %param.13, bf16[16,192,2048]{2,1,0:T(8,128)(2,1)} %param.10, f32[2048]{0:T(1024)S(1)} %convert_element_type.64, f32[16,192]{1,0:T(8,128)S(1)} %add_rsqrt_fusion.1), kind=kOutput, calls=%fused_computation.38 | convolution fusion | flops 38679871488 | bytes 62935040 | tf_op jit(solution)/shard_map/bsd,dhk->bshk/dot_general | solution.py:32
  76.9 10.2 multiply_reduce_fusion.3
  87.1 2.7 copy-done.2
  89.8 0.7 fusion.74
  90.6 0.0 copy-start.41
  90.6 0.0 slice-start
  90.6 10.4 convolution_convert_fusion.1
  101.1 10.0 convolution_convert_fusion.2
  111.1 4.3 fusion.107
  115.4 0.0 copy-start.12
  115.4 31.3 %fusion.73 = f32[16,16,192,192]{2,3,1,0:T(8,128)} fusion(bf16[16,192,16,128]{3,1,2,0:T(8,128)(2,1)} %convolution_convert_fusion.2, f32[16,192,16,192]{1,3,2,0:T(8,128)} %fusion.38), kind=kOutput, calls=%fused_computation.70 | convolution fusion | flops 2415919104 | bytes 67108864 | tf_op jit(solution)/shard_map/bqhk,bthk->bhqt/dot_general | solution.py:32
  146.7 9.6 subtract_convert_fusion.1
  156.3 0.9 subtract_convert_fusion.3
  157.2 32.2 %fusion.68 = bf16[16,192,16,128]{3,1,2,0:T(8,128)(2,1)} fusion(bf16[16,128,2048]{2,1,0:T(8,128)(2,1)} %param.19, bf16[16,192,2048]{2,1,0:T(8,128)(2,1)} %param.11), kind=kOutput, calls=%fused_computation.69 | convolution fusion | flops 25776095232 | bytes 33554432 | tf_op jit(solution)/shard_map/bsd,hkd->bshk/dot_general | solution.py:32
  189.4 31.6 %fusion.134 = f32[16,16,192,192]{2,3,1,0:T(8,128)} fusion(bf16[16,192,16,128]{3,1,2,0:T(8,128)(2,1)} %fusion.68, bf16[16,192,16,128]{3,1,2,0:T(8,128)(2,1)} %convolution_convert_fusion.1), kind=kOutput, calls=%fused_computation.138 | convolution fusion | flops 2415919104 | bytes 62914560 | tf_op jit(solution)/shard_map/bqhk,bthk->bhqt/dot_general | solution.py:32
  220.9 44.8 %fusion.133 = (f32[16,16,192]{2,1,0:T(8,128)S(1)}, f32[16,16,192,192]{2,3,1,0:T(8,128)}) fusion(f32[16,16,192,192]{2,3,1,0:T(8,128)} %fusion.73, pred[192,192]{0,1:T(8,128)(4,1)S(1)} %copy-done.32, bf16[16,192,16,32]{1,3,2,0:T(8,128)(2,1)} %get-tuple-element.22, bf16[16,192,16,32]{1,3,2,0:T(8,128)(2,1)} %get-tuple-element.21, ...), kind=kOutput, calls=%fused_computation.137 | convolution fusion | flops 1268514944 | bytes 82415616 | tf_op jit(solution)/shard_map/sub | solution.py:61
  265.7 25.6 %fusion.132 = bf16[16,16,192,192]{2,3,1,0:T(8,128)(2,1)} fusion(f32[16,16,192,192]{2,3,1,0:T(8,128)} %get-tuple-element.34, f32[16,16,192]{2,1,0:T(8,128)S(1)} %get-tuple-element.33), kind=kLoop, calls=%fused_computation.136 | loop fusion | flops 18874368 | bytes 56819712 | tf_op jit(solution)/shard_map/convert_element_type | solution.py:62
  291.3 65.6 %fusion.103 = f32[16,192,64]{1,2,0:T(8,128)} fusion(bf16[16,192,16,32]{1,3,2,0:T(8,128)(2,1)} %get-tuple-element.22, bf16[16,192,16,32]{1,3,2,0:T(8,128)(2,1)} %get-tuple-element.21, f32[16,16,192,192]{2,3,1,0:T(8,128)} %fusion.134, f32[16,16,192,192]{2,3,1,0:T(8,128)} %get-tuple-element.34, f32[16,16,192]{2,1,0:T(8,128)S(1)} %get-tuple-element.33), kind=kOutput, calls=%fused_computation.94 | convolution fusion | flops 1286652160 | bytes 82771968 | tf_op jit(solution)/shard_map/bhqt,bqhe->bte/dot_general | solution.py:32
  356.9 76.7 %fusion.63 = bf16[16,16,128,192]{2,3,1,0:T(8,128)(2,1)} fusion(f32[16,16,192,192]{2,3,1,0:T(8,128)} %fusion.134, f32[16,192,16,192]{1,3,2,0:T(8,128)} %fusion.38, f32[16,16,192,192]{2,3,1,0:T(8,128)} %get-tuple-element.34, f32[16,16,192]{2,1,0:T(8,128)S(1)} %get-tuple-element.33), kind=kOutput, calls=%fused_computation.65 | convolution fusion | flops 2488320256 | bytes 231211008 | tf_op jit(solution)/shard_map/bhqt,bqhk->bthk/dot_general | solution.py:32
  433.6 72.3 %fusion.56 = f32[16,192,16,64]{1,3,2,0:T(8,128)} fusion(f32[16,16,192,192]{2,3,1,0:T(8,128)} %fusion.134, bf16[16,192,32]{1,2,0:T(8,128)(2,1)S(1)} %copy-done.21, bf16[16,192,32]{1,2,0:T(8,128)(2,1)S(1)} %copy-done.19, f32[16,16,192,192]{2,3,1,0:T(8,128)} %get-tuple-element.34, f32[16,16,192]{2,1,0:T(8,128)S(1)} %get-tuple-element.33), kind=kOutput, calls=%fused_computation.57 | convolution fusion | flops 1274855680 | bytes 88670208 | tf_op jit(solution)/shard_map/bhqt,bte->bqhe/dot_general | solution.py:32
  505.9 70.7 %convert_bitcast_fusion = bf16[16,192,16,128]{3,1,2,0:T(8,128)(2,1)} fusion(bf16[16,192,16,128]{3,1,2,0:T(8,128)(2,1)} %convolution_convert_fusion.2, f32[16,16,192,192]{2,3,1,0:T(8,128)} %fusion.134, f32[16,16,192,192]{2,3,1,0:T(8,128)} %get-tuple-element.34, f32[16,16,192]{2,1,0:T(8,128)S(1)} %get-tuple-element.33), kind=kOutput, calls=%fused_computation.56 | convolution fusion | flops 2488320256 | bytes 100859904 | tf_op jit(solution)/shard_map/bhqt,bthk->bqhk/dot_general | solution.py:32
  576.6 23.9 %convolution_convert_fusion = bf16[16,16,128,192]{2,3,1,0:T(8,128)(2,1)} fusion(bf16[16,16,192,192]{2,3,1,0:T(8,128)(2,1)} %fusion.132, bf16[16,192,16,128]{3,1,2,0:T(8,128)(2,1)} %fusion.68), kind=kOutput, calls=%fused_computation.66 | convolution fusion | flops 2422210560 | bytes 44040192 | tf_op jit(solution)/shard_map/bhqt,bqhk->bthk/dot_general | solution.py:32
  600.5 11.8 fusion.44
  612.3 8.2 fusion.88
  620.5 19.2 %fusion.171 = bf16[16,192,16,128]{3,1,0,2:T(8,128)(2,1)} fusion(bf16[16,16,192,192]{2,3,1,0:T(8,128)(2,1)} %fusion.132, bf16[16,192,16,128]{3,1,2,0:T(8,128)(2,1)} %convolution_convert_fusion.1), kind=kOutput, calls=%fused_computation.41.clone.1 | convolution fusion | flops 2422210560 | bytes 44040192 | tf_op jit(solution)/shard_map/bhqt,bthk->bqhk/dot_general | solution.py:32
  639.7 1.0 add_convert_fusion.2
  640.7 12.1 fusion.85
  652.8 14.4 multiply_reduce_fusion.1
  667.3 0.6 broadcast_multiply_fusion
  667.9 9.5 add_convert_fusion
  677.4 11.6 copy.57
  689.0 11.7 copy.56
  700.7 59.7 %fusion.59 = f32[2048,16,192]{0,2,1:T(8,128)} fusion(bf16[16,192,16,32]{3,1,2,0:T(8,128)(2,1)} %copy.57, bf16[16,192,16,32]{3,1,2,0:T(8,128)(2,1)} %copy.56, bf16[16,192,16,128]{3,1,2,0:T(8,128)(2,1)} %convert_bitcast_fusion, bf16[16,192,2048]{2,1,0:T(8,128)(2,1)} %param.10, f32[2048]{0:T(1024)S(1)} %copy-done.29, f32[16,192]{1,0:T(8,128)S(1)} %copy-done.26), kind=kOutput, calls=%fused_computation.58 | convolution fusion | flops 38736494592 | bytes 56643584 | tf_op jit(solution)/shard_map/bsd,bshk->dhk/dot_general | solution.py:32
  760.4 34.7 %copy.63 = f32[2048,16,192]{2,1,0:T(8,128)} copy(f32[2048,16,192]{0,2,1:T(8,128)} %fusion.59) | data formatting | bytes 50331648 | tf_op jit(solution)/shard_map/bsd,bshk->dhk/dot_general | solution.py:32
  795.1 33.6 %reshape.150 = f32[6291456]{0:T(1024)} reshape(f32[2048,16,192]{2,1,0:T(8,128)} %copy.63) | data formatting | bytes 50331648 | tf_op jit(solution)/shard_map/reshape | solution.py:98
  828.8 5.6 multiply_convert_fusion.1
  834.4 2.5 copy-done.1
  837.0 7.2 convolution_bitcast_fusion.1
  844.1 3.1 copy.94
  847.2 5.9 convolution_bitcast_fusion
  853.1 1.0 reshape.152
  854.1 6.6 copy.66
  860.6 6.6 copy.68
  867.3 32.0 %fusion.40 = f32[16,128,2048,1]{2,1,3,0:T(8,128)S(1)} fusion(bf16[16,192,2048]{2,1,0:T(8,128)(2,1)} %param.11, bf16[16,192,16,128]{3,1,0,2:T(8,128)(2,1)} %fusion.171), kind=kOutput, calls=%fused_computation.40 | convolution fusion | flops 25769803776 | bytes 41943040 | tf_op jit(solution)/shard_map/bshk,bsd->hkd/dot_general | solution.py:32
  899.3 7.4 copy.95
  906.7 0.0 all-reduce.12.cloned.1.call-update
  906.7 13.6 fusion.95
  920.4 60.2 %fusion.51 = f32[16,192,2048,1]{2,1,3,0:T(8,128)} fusion(bf16[2048,16,192]{0,2,1:T(8,128)(2,1)} %param.13, bf16[16,192,16,32]{3,1,2,0:T(8,128)(2,1)} %copy.57, bf16[16,192,16,32]{3,1,2,0:T(8,128)(2,1)} %copy.56, bf16[16,192,16,128]{3,1,2,0:T(8,128)(2,1)} %convert_bitcast_fusion), kind=kOutput, calls=%fused_computation.51 | convolution fusion | flops 38711328768 | bytes 56623104 | tf_op jit(solution)/shard_map/bshk,dhk->bsd/dot_general | solution.py:32
  980.6 30.6 %fusion.17 = (f32[2048]{0:T(1024)S(1)}, f32[16,192]{1,0:T(8,128)S(1)}, f32[16,192,2048]{2,1,0:T(8,128)}) fusion(bf16[16,192,2048]{2,1,0:T(8,128)(2,1)} %param.10, f32[16,192]{1,0:T(8,128)S(1)} %copy-done.27, f32[2048]{0:T(1024)S(1)} %copy-done.30, bf16[2048,64]{0,1:T(8,128)(2,1)S(1)} %copy-done.17, bf16[16,192,32]{1,2,0:T(8,128)(2,1)S(1)} %copy-done.10, ...), kind=kOutput, calls=%fused_computation.22 | convolution fusion | flops 862710784 | bytes 88776704 | tf_op jit(solution)/shard_map/bse,de->bsd/dot_general | solution.py:32
  1011.3 43.4 %all-reduce.8 = (f32[2048]{0:T(1024)S(1)}, f32[512]{0:T(512)S(1)}) all-reduce(f32[2048]{0:T(1024)S(1)} %get-tuple-element.9, f32[512]{0:T(512)S(1)} %copy-done.37), channel_id=2, replica_groups=mesh['dp'=32] {'dp'}, use_global_device_ids=true, to_apply=%region_8.9.clone | all-reduce | flops 2560 | bytes 20480
  1054.6 0.6 dynamic-slice_multiply_fusion.7
  1055.2 0.6 dynamic-slice_multiply_fusion.6
  1055.8 21.5 %fusion.16 = bf16[16,192,2048]{2,1,0:T(8,128)(2,1)} fusion(bf16[16,192,2048]{2,1,0:T(8,128)(2,1)} %param.10, bf16[16,192,2048]{2,1,0:T(8,128)(2,1)} %param.11, f32[16,192,2048]{2,1,0:T(8,128)} %get-tuple-element.36, f32[16,192]{1,0:T(8,128)S(1)} %broadcast_multiply_fusion.1, f32[2048]{0:T(1024)S(1)} %copy-done.30, f32[16,192]{1,0:T(8,128)S(1)} %copy-done.27), kind=kLoop, calls=%fused_computation.21 | loop fusion | flops 56623104 | bytes 62947328 | tf_op jit(solution)/shard_map/convert_element_type | solution.py:89
  1077.3 613.4 %all-reduce.12.cloned.1.call-done = (f32[6291456]{0:T(1024)}, f32[1048576]{0:T(1024)}, f32[131072]{0:T(1024)}, f32[1048576]{0:T(1024)}, f32[1048576]{0:T(1024)}, /*index=5*/f32[4194304]{0:T(1024)}) async-done(((f32[6291456]{0:T(1024)}, f32[1048576]{0:T(1024)}, f32[131072]{0:T(1024)}, f32[1048576]{0:T(1024)}, f32[1048576]{0:T(1024)}, /*index=5*/f32[4194304]{0:T(1024)}), (f32[6291456]{0:T(1024)}, ...) | async-done | bytes 55050256
  1690.7 2.1 dynamic-slice_multiply_fusion
  1692.7 1.6 dynamic-slice_multiply_fusion.4
  1694.3 1.3 dynamic-slice_multiply_fusion.5
  1695.6 1.7 dynamic-slice_multiply_fusion.2
  1697.3 1.9 dynamic-slice_multiply_fusion.1
  (98 shorter events, 0.2 us)
Async XLA Ops:
  7.2 69.7 %copy-start = (bf16[2048,512]{1,0:T(8,128)(2,1)S(1)}, bf16[2048,512]{1,0:T(8,128)(2,1)}, u32[]{:S(2)}) copy-start(bf16[2048,512]{1,0:T(8,128)(2,1)} %param.14) | copy-start | bytes 6291460
  7.2 7.8 copy-start.36
  7.2 1683.5 %all-reduce.12.cloned.1.call-start = ((), (), s32[]{:S(2)}) async-start(), calls=%async_computation | async-start | bytes 110100480
  15.0 96.0 %copy-start.25 = (f32[16,192]{1,0:T(8,128)}, f32[16,192]{1,0:T(8,128)S(1)}, u32[]{:S(2)}) copy-start(f32[16,192]{1,0:T(8,128)S(1)} %add_rsqrt_fusion.1) | copy-start | bytes 36868
  15.1 96.0 %copy-start.28 = (f32[2048]{0:T(1024)}, f32[2048]{0:T(1024)S(1)}, u32[]{:S(2)}) copy-start(f32[2048]{0:T(1024)S(1)} %convert_element_type.64) | copy-start | bytes 24580
  76.9 10.2 copy-start.38
  76.9 13.7 copy-start.39
  87.1 2.7 copy-start.2
  87.1 3.4 copy-start.33
  87.1 2.7 copy-start.22
  90.6 10.5 copy-start.4
  90.6 10.5 copy-start.41
  90.6 20.5 %slice-start = ((s8[12582912]{0:T(1024)(128)(4,1)}), s8[4194304]{0:T(1024)(128)(4,1)S(1)}, s32[]{:S(2)}) async-start(s8[12582912]{0:T(1024)(128)(4,1)} %bitcast.179), calls=%async_computation.1 | async-start | bytes 8388608
  90.6 20.5 %slice-start.1 = ((s8[12582912]{0:T(1024)(128)(4,1)}), s8[4194304]{0:T(1024)(128)(4,1)S(1)}, s32[]{:S(2)}) async-start(s8[12582912]{0:T(1024)(128)(4,1)} %bitcast.179), calls=%async_computation.2 | async-start | bytes 8388608
  101.0 10.0 slice-start.2
  101.0 10.1 copy-start.16
  115.4 31.3 %copy-start.12 = (f32[192,32]{0,1:T(8,128)S(1)}, f32[192,32]{0,1:T(8,128)}, u32[]{:S(2)}) copy-start(f32[192,32]{0,1:T(8,128)} %get-tuple-element.29) | copy-start | bytes 73732
  115.4 31.3 %copy-start.14 = (f32[192,32]{0,1:T(8,128)S(1)}, f32[192,32]{0,1:T(8,128)}, u32[]{:S(2)}) copy-start(f32[192,32]{0,1:T(8,128)} %get-tuple-element.30) | copy-start | bytes 73732
  157.2 63.7 %copy-start.18 = (bf16[16,192,32]{1,2,0:T(8,128)(2,1)}, bf16[16,192,32]{1,2,0:T(8,128)(2,1)S(1)}, u32[]{:S(2)}) copy-start(bf16[16,192,32]{1,2,0:T(8,128)(2,1)S(1)} %get-tuple-element.27) | copy-start | bytes 589828
  189.4 31.6 %copy-start.20 = (bf16[16,192,32]{1,2,0:T(8,128)(2,1)S(1)}, bf16[16,192,32]{1,2,0:T(8,128)(2,1)}, u32[]{:S(2)}) copy-start(bf16[16,192,32]{1,2,0:T(8,128)(2,1)} %get-tuple-element.28) | copy-start | bytes 589828
  189.4 31.6 %copy-start.32 = (pred[192,192]{0,1:T(8,128)(4,1)S(1)}, pred[192,192]{0,1:T(8,128)(4,1)}, u32[]{:S(2)}) copy-start(pred[192,192]{0,1:T(8,128)(4,1)} %iota_compare_fusion) | copy-start | bytes 110596
  356.9 76.7 %copy-start.19 = (bf16[16,192,32]{1,2,0:T(8,128)(2,1)S(1)}, bf16[16,192,32]{1,2,0:T(8,128)(2,1)}, u32[]{:S(2)}) copy-start(bf16[16,192,32]{1,2,0:T(8,128)(2,1)} %copy-done.18) | copy-start | bytes 589828
  356.9 76.7 %copy-start.21 = (bf16[16,192,32]{1,2,0:T(8,128)(2,1)S(1)}, bf16[16,192,32]{1,2,0:T(8,128)(2,1)}, u32[]{:S(2)}) copy-start(bf16[16,192,32]{1,2,0:T(8,128)(2,1)} %get-tuple-element.28) | copy-start | bytes 589828
  576.6 23.9 %copy-start.40 = (bf16[512,16,128]{2,1,0:T(8,128)(2,1)S(1)}, bf16[512,16,128]{2,1,0:T(8,128)(2,1)}, u32[]{:S(2)}) copy-start(bf16[512,16,128]{2,1,0:T(8,128)(2,1)} %param.18) | copy-start | bytes 6291460
  600.5 11.8 copy-start.3
  600.5 11.8 copy-start.5
  620.5 19.3 %copy-start.11 = (f32[16,192,64]{1,2,0:T(8,128)S(1)}, f32[16,192,64]{1,2,0:T(8,128)}, u32[]{:S(2)}) copy-start(f32[16,192,64]{1,2,0:T(8,128)} %fusion.103) | copy-start | bytes 2359300
  620.5 19.3 %copy-start.13 = (f32[192,32]{0,1:T(8,128)S(1)}, f32[192,32]{0,1:T(8,128)}, u32[]{:S(2)}) copy-start(f32[192,32]{0,1:T(8,128)} %get-tuple-element.29) | copy-start | bytes 73732
  620.5 19.3 %copy-start.15 = (f32[192,32]{0,1:T(8,128)S(1)}, f32[192,32]{0,1:T(8,128)}, u32[]{:S(2)}) copy-start(f32[192,32]{0,1:T(8,128)} %get-tuple-element.30) | copy-start | bytes 73732
  620.5 32.3 %slice-start.3 = ((s8[6291456]{0:T(1024)(128)(4,1)}), s8[2097152]{0:T(1024)(128)(4,1)S(1)}, s32[]{:S(2)}) async-start(s8[6291456]{0:T(1024)(128)(4,1)} %bitcast.182), calls=%async_computation.4 | async-start | bytes 4194304
  640.7 12.1 slice-start.4
  640.7 12.1 copy-start.23
  640.7 12.1 copy-start.34
  640.7 12.1 copy-start.42
  689.0 11.7 copy-start.26
  689.0 11.7 copy-start.29
  795.1 33.7 %copy-start.24 = (f32[16,192]{1,0:T(8,128)S(1)}, f32[16,192]{1,0:T(8,128)}, u32[]{:S(2)}) copy-start(f32[16,192]{1,0:T(8,128)} %copy-done.22) | copy-start | bytes 36868
  795.1 33.7 %copy-start.31 = (f32[16,192]{1,0:T(8,128)S(1)}, f32[16,192]{1,0:T(8,128)}, u32[]{:S(2)}) copy-start(f32[16,192]{1,0:T(8,128)} %broadcast_multiply_fusion) | copy-start | bytes 36868
  795.1 33.7 %copy-start.35 = (f32[512]{0:T(512)S(1)}, f32[512]{0:T(512)}, u32[]{:S(2)}) copy-start(f32[512]{0:T(512)} %copy-done.33) | copy-start | bytes 6148
  828.7 8.2 copy-start.1
  836.9 7.2 copy-start.6
  837.0 10.2 copy-start.7
  837.0 10.2 copy-start.9
  920.3 60.2 %copy-start.8 = (bf16[16,192,32]{1,2,0:T(8,128)(2,1)S(1)}, bf16[16,192,32]{1,2,0:T(8,128)(2,1)}, u32[]{:S(2)}) copy-start(bf16[16,192,32]{1,2,0:T(8,128)(2,1)} %get-tuple-element.25) | copy-start | bytes 589828
  920.4 60.2 %copy-start.10 = (bf16[16,192,32]{1,2,0:T(8,128)(2,1)S(1)}, bf16[16,192,32]{1,2,0:T(8,128)(2,1)}, u32[]{:S(2)}) copy-start(bf16[16,192,32]{1,2,0:T(8,128)(2,1)} %get-tuple-element.26) | copy-start | bytes 589828
  920.4 60.2 %copy-start.17 = (bf16[2048,64]{0,1:T(8,128)(2,1)S(1)}, bf16[2048,64]{0,1:T(8,128)(2,1)}, u32[]{:S(2)}) copy-start(bf16[2048,64]{0,1:T(8,128)(2,1)} %param.16) | copy-start | bytes 786436
  920.4 60.2 %copy-start.27 = (f32[16,192]{1,0:T(8,128)S(1)}, f32[16,192]{1,0:T(8,128)}, u32[]{:S(2)}) copy-start(f32[16,192]{1,0:T(8,128)} %copy-done.25) | copy-start | bytes 36868
  920.4 60.2 %copy-start.30 = (f32[2048]{0:T(1024)S(1)}, f32[2048]{0:T(1024)}, u32[]{:S(2)}) copy-start(f32[2048]{0:T(1024)} %copy-done.28) | copy-start | bytes 24580
  980.6 30.6 %copy-start.37 = (f32[512]{0:T(512)S(1)}, f32[512]{0:T(512)}, u32[]{:S(2)}) copy-start(f32[512]{0:T(512)} %get-tuple-element.11) | copy-start | bytes 6148
Sparse Core Ops, SparseCore 0:
  906.8 783.7 all-reduce.11
where the time goes:
time: 1720 us; the launch traced here: 1710 us
  matrix products  820 us (48%)
  waiting for transfers between devices  613 us (36%)
  local copies, waits for them, and re-layouts  122 us (7%)
  other arithmetic  93.4 us (5%)
  blocking collectives  43.4 us (3%)
    dot_general x25, matrix products, contract(): jnp.einsum(eq_form, operand_a, operand_b, preferred_element_type=jnp.floa...  775 us
    unnamed x2, waiting for transfers between devices  613 us
    dot_general x3, local copies, waits for them, and re-layouts, contract(): jnp.einsum(eq_form, operand_a, operand_b, preferred_element_type=jnp.floa...  47.9 us
    sub x1, matrix products, block_grads(): attn_prob = jax.nn.softmax(jnp.where(causal, scores, -1e+30), axis=-1)  44.8 us
    unnamed x1, blocking collectives  43.4 us
    reshape x2, local copies, waits for them, and re-layouts, device_step(): local_grad.reshape(-1)  34.6 us
  transfers between devices with their start and end apart: 1, of which 1 were waited for; matrix products, arithmetic and copies ran while one was open for 7% of the time, Pallas kernels for 0%

commit v1 on v0

v1 whole, which is shorter than its diff:
```python
import functools

import jax
import jax.numpy as jnp
from jax import lax
from jax.experimental import pallas as pl
from jax.experimental.pallas import tpu as pltpu
from jax.sharding import PartitionSpec as P

EPS = 1e-6
ROPE_BASE = 10000.0
GROUPS = 2
BITS = ('c', 'x', 'y', 'z0', 'z1')


def contract(operand_a, operand_b, dim_a, dim_b):
    return lax.dot_general(operand_a, operand_b, (((dim_a,), (dim_b,)), ((), ())),
                           preferred_element_type=jnp.float32)


def rope_tables(seq_len, rot_dim):
    half_dim = rot_dim // 2
    inv_freq = jnp.power(ROPE_BASE, -2.0 * jnp.arange(half_dim, dtype=jnp.float32) / rot_dim)
    angles = jnp.arange(seq_len, dtype=jnp.float32)[:, None] * inv_freq[None, :]
    cos_t, sin_t = jnp.cos(angles), jnp.sin(angles)
    return jnp.concatenate([cos_t] * 4, axis=-1), jnp.concatenate([-sin_t, sin_t] * 2, axis=-1)


def swap_halves(vals, is_first):
    return jnp.where(is_first, pltpu.roll(vals, 96, 1), pltpu.roll(vals, 32, 1))


def split_cores(even, odd, low_half, first_core):
    low = jnp.where(low_half, even, pltpu.roll(odd, 64, 1)).astype(jnp.bfloat16)
    high = jnp.where(low_half, pltpu.roll(even, 64, 1), odd).astype(jnp.bfloat16)
    return jnp.where(first_core, high, low), jnp.where(first_core, low, high)


def norm_body(core_ref, x_ref, gain_ref, hidden_ref, send_ref, keep_ref):
    x_wide = x_ref[...].astype(jnp.float32)
    rows = x_wide.shape[0]
    inv_x = lax.rsqrt(jnp.mean(x_wide * x_wide, axis=-1, keepdims=True) + EPS)
    hidden = x_wide * inv_x * gain_ref[...]
    hidden_ref[...] = hidden.astype(jnp.bfloat16)
    low_half = lax.broadcasted_iota(jnp.int32, (rows, 128), 1) < 64
    for pair in range(hidden.shape[1] // 256):
        cols = slice(128 * pair, 128 * pair + 128)
        send_ref[:, cols], keep_ref[:, cols] = split_cores(
            hidden[:, 256 * pair:256 * pair + 128], hidden[:, 256 * pair + 128:256 * pair + 256], low_half, core_ref[0] == 0)


def normalize(core, x_in, gain, block=256):
    tokens, dim = x_in.shape

    def rows(width):
        return pl.BlockSpec((block, width), lambda i: (i, 0))

    return pl.pallas_call(
        norm_body,
        grid=(tokens // block,),
        in_specs=[pl.BlockSpec(memory_space=pltpu.SMEM), rows(dim), pl.BlockSpec((1, dim), lambda i: (0, 0))],
        out_specs=[rows(dim), rows(dim // 2), rows(dim // 2)],
        out_shape=[jax.ShapeDtypeStruct((tokens, width), jnp.bfloat16) for width in (dim, dim // 2, dim // 2)],
        compiler_params=pltpu.CompilerParams(dimension_semantics=('arbitrary',), vmem_limit_bytes=48 * 1024 * 1024),
        cost_estimate=pl.CostEstimate(flops=tokens * dim * 8, bytes_accessed=tokens * dim * 6, transcendentals=0),
    )(core, x_in, gain)


def attn_body(heads, qk_scale, core_ref, qn_ref, qr_ref, kr_ref, kn_ref, v_ref, do_ref, cos_ref, sin_ref,
              send_ref, keep_ref, dq_ref, dkv_ref, dkr_ref):
    seq_len = qn_ref.shape[0]
    lane = lax.broadcasted_iota(jnp.int32, (seq_len, 128), 1)
    is_first = (lane % 64) < 32
    low_half = lane < 64
    cos_t, sin_t = cos_ref[...], sin_ref[...]
    key_pos = lax.broadcasted_iota(jnp.int32, (seq_len, seq_len), 0)
    query_pos = lax.broadcasted_iota(jnp.int32, (seq_len, seq_len), 1)
    causal = key_pos <= query_pos
    kr_raw = kr_ref[...]
    k_rot = kr_raw * cos_t + swap_halves(kr_raw, is_first) * sin_t
    k_half = (jnp.where(low_half, k_rot, 0.0).astype(jnp.bfloat16), jnp.where(low_half, 0.0, k_rot).astype(jnp.bfloat16))
    dkr_sum = [None, None]
    for pair in range(heads // 2):
        rot_cols = slice(128 * pair, 128 * pair + 128)
        q_raw = qr_ref[:, rot_cols]
        q_rot = (q_raw * cos_t + swap_halves(q_raw, is_first) * sin_t).astype(jnp.bfloat16)
        dq_rot, outs = None, []
        for side in range(2):
            head = 2 * pair + side
            cols = slice(128 * head, 128 * head + 128)
            q_cat = jnp.concatenate([qn_ref[:, cols], q_rot], axis=1)
            k_cat = jnp.concatenate([kn_ref[:, cols], k_half[side]], axis=1)
            v_head = v_ref[:, cols]
            do_head = do_ref[:, cols]
            scores = jnp.where(causal, contract(k_cat, q_cat, 1, 1) * qk_scale, -1e30)
            expo = jnp.exp(scores - jnp.max(scores, axis=0, keepdims=True))
            prob = expo * (1.0 / jnp.sum(expo, axis=0, keepdims=True))
            prob_low = prob.astype(jnp.bfloat16)
            outs.append(contract(prob_low, v_head, 0, 0))
            d_prob = contract(v_head, do_head, 1, 1)
            row_dot = jnp.sum(prob * d_prob, axis=0, keepdims=True)
            d_scores = (prob * (d_prob - row_dot) * qk_scale).astype(jnp.bfloat16)
            d_v = contract(prob_low, do_head, 1, 0)
            d_k = contract(d_scores, q_cat, 1, 0)
            d_q = contract(d_scores, k_cat, 0, 0)
            dkv_ref[:, cols] = d_k[:, :128].astype(jnp.bfloat16)
            dkv_ref[:, slice(128 * (heads + head), 128 * (heads + head) + 128)] = d_v.astype(jnp.bfloat16)
            dq_ref[:, cols] = d_q[:, :128].astype(jnp.bfloat16)
            dq_rot = d_q[:, 128:] if dq_rot is None else dq_rot + d_q[:, 128:]
            dkr_sum[side] = d_k[:, 128:] if dkr_sum[side] is None else dkr_sum[side] + d_k[:, 128:]
        send_ref[:, rot_cols], keep_ref[:, rot_cols] = split_cores(outs[0], outs[1], low_half, core_ref[0] == 0)
        dq_back = dq_rot * cos_t - swap_halves(dq_rot, is_first) * sin_t
        dq_ref[:, slice(128 * heads + 128 * pair, 128 * heads + 128 * pair + 128)] = dq_back.astype(jnp.bfloat16)
    dk_rot = dkr_sum[0] + pltpu.roll(dkr_sum[1], 64, 1)
    dkr_ref[...] = dk_rot * cos_t - swap_halves(dk_rot, is_first) * sin_t


def attention(n_seq, seq_len, heads, qk_scale, core, q_nope, q_raw, k_raw, k_nope, v_heads, d_attn, cos_t, sin_t):
    tokens = n_seq * seq_len

    def rows(width):
        return pl.BlockSpec((seq_len, width), lambda i: (i, 0))

    table = pl.BlockSpec((seq_len, 128), lambda i: (0, 0))
    wide = heads * 128
    flops = n_seq * heads * seq_len * seq_len * 2 * (256 * 3 + 128 * 3)
    return pl.pallas_call(
        functools.partial(attn_body, heads, qk_scale),
        grid=(n_seq,),
        in_specs=[pl.BlockSpec(memory_space=pltpu.SMEM), rows(wide), rows(heads * 64), rows(128), rows(wide), rows(wide), rows(wide), table, table],
        out_specs=[rows(wide // 2), rows(wide // 2), rows(heads * 192), rows(2 * wide), rows(128)],
        out_shape=[jax.ShapeDtypeStruct((tokens, wide // 2), jnp.bfloat16),
                   jax.ShapeDtypeStruct((tokens, wide // 2), jnp.bfloat16),
                   jax.ShapeDtypeStruct((tokens, heads * 192), jnp.bfloat16),
                   jax.ShapeDtypeStruct((tokens, 2 * wide), jnp.bfloat16),
                   jax.ShapeDtypeStruct((tokens, 128), jnp.float32)],
        compiler_params=pltpu.CompilerParams(dimension_semantics=('arbitrary',), vmem_limit_bytes=48 * 1024 * 1024),
        cost_estimate=pl.CostEstimate(flops=flops, bytes_accessed=tokens * wide * 20, transcendentals=0),
    )(core, q_nope, q_raw, k_raw, k_nope, v_heads, d_attn, cos_t, sin_t)


def tail_body(n_in, n_weights, *refs):
    acts, weights = refs[:n_in], refs[n_in:n_in + n_weights]
    x_ref, gy_ref, gain_ref, gx_ref, dg_ref = refs[n_in + n_weights:n_in + n_weights + 3] + refs[-2:]
    blocks = [(act, start) for act, starts in zip(acts, ((0, 1024), (0, 1024), (0,))) for start in starts]
    d_hidden = None
    for (act, start), weight in zip(blocks, weights):
        term = contract(act[:, start:start + weight.shape[0]], weight[...], 1, 0)
        d_hidden = term if d_hidden is None else d_hidden + term
    x_wide = x_ref[...].astype(jnp.float32)
    inv_x = lax.rsqrt(jnp.mean(x_wide * x_wide, axis=-1, keepdims=True) + EPS)
    x_hat = x_wide * inv_x
    prod = d_hidden * x_hat
    gain = gain_ref[...]

    @pl.when(pl.program_id(0) == 0)
    def _():
        dg_ref[...] = jnp.zeros_like(dg_ref)

    dg_ref[...] += jnp.sum(prod, axis=0, keepdims=True)
    mean_dot = jnp.mean(prod * gain, axis=-1, keepdims=True)
    grad_x = gy_ref[...].astype(jnp.float32) + inv_x * (d_hidden * gain - x_hat * mean_dot)
    gx_ref[...] = grad_x.astype(jnp.bfloat16)


def tail(acts, weights, x_in, grad_y, gain, start, tokens, before, block=256):
    dim = x_in.shape[1]
    first = start // block

    def rows(width):
        return pl.BlockSpec((block, width), lambda i: (i + first, 0))

    def whole(arr):
        return pl.BlockSpec(arr.shape, lambda i: (0, 0), pipeline_mode=pl.Buffered(1))

    width = sum(act.shape[1] for act in acts)
    return pl.pallas_call(
        functools.partial(tail_body, len(acts), len(weights)),
        grid=(tokens // block,),
        in_specs=[rows(act.shape[1]) for act in acts] + [whole(weight) for weight in weights]
        + [rows(dim), rows(dim), pl.BlockSpec((1, dim), lambda i: (0, 0))] + [pl.BlockSpec(memory_space=pl.ANY)] * len(before),
        out_specs=[rows(dim), pl.BlockSpec((1, dim), lambda i: (0, 0))],
        input_output_aliases={len(acts) + len(weights) + 3: 0} if before else {},
        out_shape=[jax.ShapeDtypeStruct(x_in.shape, jnp.bfloat16), jax.ShapeDtypeStruct((1, dim), jnp.float32)],
        compiler_params=pltpu.CompilerParams(dimension_semantics=('arbitrary',), vmem_limit_bytes=58 * 1024 * 1024),
        cost_estimate=pl.CostEstimate(flops=2 * tokens * dim * width, bytes_accessed=tokens * (2 * width + 6 * dim) + 2 * width * dim,
                                      transcendentals=0),
    )(*acts, *weights, x_in, grad_y, gain, *before)


def solution(mesh):
    n_dev = mesh.shape['dp']
    perms = {name: [(dev, dev ^ (1 << pos)) for dev in range(n_dev)] for pos, name in enumerate(BITS)}

    def device_step(x_in, grad_y, g_in, w_q, w_dkv, g_kv, w_kr, w_uk, w_uv, w_o):
        me = lax.axis_index('dp')
        bit = {name: (me >> pos) & 1 for pos, name in enumerate(BITS)}

        def pick(arr, axis, index):
            return lax.dynamic_index_in_dim(arr, index, axis, keepdims=False)

        def exchange(addends, dims, name):
            axis = dims.index(name)
            send = sum(pick(arr, axis, 1 - bit[name]) for arr in addends)
            return send, [pick(arr, axis, bit[name]) for arr in addends], dims[:axis] + dims[axis + 1:]

        class Stream:
            def __init__(self, addends, dims, order):
                self.lanes, self.later = [(addends, dims, order)], ()
                self.fork()

            def sends(self):
                steps = [exchange(addends, dims, order[0]) for addends, dims, order in self.lanes]
                self.held = [(keep, dims, lane[2][0], lane[2][1:]) for (_, keep, dims), lane in zip(steps, self.lanes)]
                return [step[0] for step in steps]

            def transfer(self, values):
                return [lax.ppermute(value, 'dp', perms[held[2]]) for value, held in zip(values, self.held)]

            def receive(self, values):
                self.lanes = [(keep + [value], dims, order) for (keep, dims, _, order), value in zip(self.held, values)]
                self.fork()

            def fork(self):
                if len(self.lanes) == 1 and self.lanes[0][2] == () and 'x' in self.lanes[0][1]:
                    addends, dims, _ = self.lanes[0]
                    later = tuple(name for name in BITS[3:] if name in dims)
                    split = (addends[0].shape[-1] // 256) * 128
                    self.lanes = [([part[..., :split] for part in addends], dims, ('x', 'y') + later),
                                  ([part[..., split:] for part in addends], dims, ('y', 'x') + later)]

            def active(self):
                return bool(self.lanes[0][2])

            def result(self):
                return jnp.concatenate([sum(addends) for addends, _, _ in self.lanes], axis=-1)

        streams = []

        def launch(arr, names, order=()):
            rows = arr.shape[0] // (1 << len(names))
            streams.append(Stream([arr.reshape((2,) * len(names) + (rows, arr.shape[1]))], tuple(reversed(names)), order))
            return streams[-1]

        class Pair(Stream):
            def __init__(self, arr):
                self.value, self.open = arr, True
                streams.append(self)

            def sends(self):
                return [self.value]

            def transfer(self, values):
                return [lax.ppermute(values[0], 'dp', perms['c'])]

            def receive(self, values):
                self.value, self.open = values[0], False

            def active(self):
                return self.open

        def tick(work, *inputs):
            live = [stream for stream in streams if stream.active()]
            sends = [stream.sends() for stream in live]
            inputs, sends = lax.optimization_barrier((inputs, sends))
            arrived = [stream.transfer(values) for stream, values in zip(live, sends)]
            outs, arrived = lax.optimization_barrier((work(*inputs), arrived))
            for stream, values in zip(live, arrived):
                stream.receive(values)
            return outs

        def drain():
            while any(stream.active() for stream in streams):
                for stream in streams:
                    if stream.active():
                        stream.receive(stream.transfer(stream.sends()))

        n_seq, seq_len, dim = x_in.shape
        tokens = n_seq * seq_len
        heads, nope = w_uk.shape[1], w_uk.shape[2]
        rank = w_dkv.shape[1]
        rot = w_kr.shape[1]
        qk_scale = w_q.shape[2] ** -0.5
        group = heads // GROUPS
        cos_t, sin_t = rope_tables(seq_len, rot)
        x2 = x_in.reshape(tokens, dim)
        gy2 = grad_y.reshape(tokens, dim)
        gain_in = g_in.astype(jnp.float32)
        gain_kv = g_kv.astype(jnp.float32)
        core = bit['c'].astype(jnp.int32).reshape(1)
        hidden, h_send, h_keep = normalize(core, x2, gain_in[None, :])
        w_side = jnp.concatenate([w_dkv, w_kr, w_kr], axis=1)
        side = contract(hidden, w_side, 1, 0)
        latent, k_raw = side[:, :rank], side[:, rank:]
        inv_lat = lax.rsqrt(jnp.mean(latent * latent, axis=-1, keepdims=True) + EPS)
        lat_hat = latent * inv_lat
        lat_norm = (lat_hat * gain_kv).astype(jnp.bfloat16)
        w_o2 = w_o.reshape(heads * nope, dim)

        lat_norm = lax.optimization_barrier(lat_norm)
        w_groups, w_parts = [], []
        for g in range(GROUPS):
            hs = slice(g * group, (g + 1) * group)
            w_nope = w_q[:, hs, :nope].reshape(dim, group * nope)
            w_rot = w_q[:, hs, nope:].reshape(dim, group * rot)
            w_groups.extend([w_nope.T, w_rot.T])
            w_parts.append((w_nope, w_rot, w_uk[:, hs].reshape(rank, group * nope), w_uv[:, hs].reshape(rank, group * nope),
                            w_o2[g * group * nope:(g + 1) * group * nope]))

        def project_q(g, hidden):
            return (contract(hidden, w_parts[g][0], 1, 0).astype(jnp.bfloat16), contract(hidden, w_parts[g][1], 1, 0))

        def project_kv(g, lat_norm, gy2):
            return (contract(lat_norm, w_parts[g][2], 1, 0).astype(jnp.bfloat16),
                    contract(lat_norm, w_parts[g][3], 1, 0).astype(jnp.bfloat16),
                    contract(gy2, w_parts[g][4], 1, 1).astype(jnp.bfloat16))

        def attend(q_nope, q_raw, k_raw, k_nope, v_heads, d_attn):
            return attention(n_seq, seq_len, group, qk_scale, core, q_nope, q_raw, k_raw, k_nope, v_heads, d_attn, cos_t, sin_t)

        def outer(*pairs):
            return [contract(pairs[i], pairs[i + 1], 0, 0) for i in range(0, len(pairs), 2)]

        def outer_add(left, right, received):
            return contract(left, right, 0, 0) + received

        def latent_back(d_kv0, d_kv1, dkr0, dkr1, lat_hat, inv_lat):
            d_lat = sum(contract(d_kv, jnp.concatenate(w_parts[g][2:4], axis=1), 1, 1) for g, d_kv in enumerate((d_kv0, d_kv1)))
            d_g_kv = jnp.sum(d_lat * lat_hat, axis=0)
            d_lat_hat = d_lat * gain_kv
            d_latent = inv_lat * (d_lat_hat - lat_hat * jnp.mean(d_lat_hat * lat_hat, axis=-1, keepdims=True))
            lane_ok = jnp.arange(2 * rot) < rot
            d_side = jnp.concatenate([d_latent, jnp.where(lane_ok, dkr0 + dkr1, 0.0)], axis=1).astype(jnp.bfloat16)
            return d_g_kv, d_side

        q_parts = project_q(0, hidden)
        kv_parts = project_kv(0, lat_norm, gy2)
        CHIP = BITS[1:]
        o_send, o_keep, d_q0, d_kv0, dkr0 = attend(*q_parts, k_raw, *kv_parts)
        pair_q = Pair(lax.optimization_barrier(outer(h_send, d_q0))[0])
        wo_send, d_wkv = tick(outer, o_send, gy2, lat_norm, d_kv0)
        pair_o, shards_kv = Pair(wo_send), [launch(d_wkv, BITS, ('c',))]
        shards_q = [launch(tick(outer_add, h_keep, d_q0, pair_q.value), CHIP)]
        d_wo, q_parts = tick(lambda left, right, received, hidden: (outer_add(left, right, received), project_q(1, hidden)),
                             o_keep, gy2, pair_o.value, hidden)
        shards_o = [launch(d_wo, CHIP[:3])]
        kv_parts = tick(functools.partial(project_kv, 1), lat_norm, gy2)
        o_send, o_keep, d_q1, d_kv1, dkr1 = tick(attend, *q_parts, k_raw, *kv_parts)
        pair_q = Pair(tick(outer, h_send, d_q1)[0])
        wo_send, d_wkv = tick(outer, o_send, gy2, lat_norm, d_kv1)
        pair_o = Pair(wo_send)
        shards_kv.append(launch(d_wkv, BITS, ('c',)))
        shards_q.append(launch(tick(outer_add, h_keep, d_q1, pair_q.value), CHIP))
        d_wo, (d_g_kv, d_side) = tick(lambda left, right, received, *rest: (outer_add(left, right, received), latent_back(*rest)),
                                      o_keep, gy2, pair_o.value, d_kv0, d_kv1, dkr0, dkr1, lat_hat, inv_lat)
        shards_o.append(launch(d_wo, CHIP[:3]))
        third = tokens // 3

        def tail_part(part, before, *acts):
            return tail(acts, w_groups + [w_side.T], x2, gy2, gain_in[None, :], part * third, third, before)

        d_wside, (grad_x, d_g_in) = tick(lambda hidden, *acts: (contract(hidden, acts[-1], 0, 0), tail_part(0, (), *acts)),
                                         hidden, d_q0, d_q1, d_side)
        shard_side = launch(d_wside, BITS, ('c',))
        for part in range(1, 3):
            grad_x, d_g_part = tick(lambda before, *acts: tail_part(part, (before,), *acts), grad_x, d_q0, d_q1, d_side)
            d_g_in = d_g_in + d_g_part
        small = jnp.concatenate([d_g_in.reshape(n_dev, -1), d_g_kv.reshape(n_dev, -1)], axis=1)
        small = jnp.pad(small, ((0, 0), (0, 128 - small.shape[1]))).reshape((2,) * 5 + (1, 128))
        addends, dims = [small], tuple(reversed(BITS))
        for name in BITS:
            send, keep, dims = exchange(addends, dims, name)
            addends = keep + [lax.ppermute(send, 'dp', perms[name])]
        small = sum(addends)[0] / n_dev
        drain()
        low, high = [shard.result() for shard in shards_o]
        mine = jnp.where(bit['z1'] == 0, low, high)
        d_w_o = mine + lax.ppermute(jnp.where(bit['z1'] == 0, high, low), 'dp', perms['z1'])
        shards_q = [shard.result() for shard in shards_q]
        shards_kv = [shard.result() for shard in shards_kv]
        shard_side = shard_side.result()

        per_in, per_kv = dim // n_dev, rank // n_dev
        inv_dev = 1.0 / n_dev
        q_parts = [jnp.concatenate([shard[:, :group * nope].reshape(-1, group, nope),
                                    shard[:, group * nope:].reshape(-1, group, rot)], axis=-1) for shard in shards_q]
        d_w_q = jnp.concatenate(q_parts, axis=1).reshape(-1) * inv_dev
        d_w_uk = jnp.concatenate([shard[:, :group * nope] for shard in shards_kv], axis=1).reshape(-1) * inv_dev
        d_w_uv = jnp.concatenate([shard[:, group * nope:] for shard in shards_kv], axis=1).reshape(-1) * inv_dev
        return (grad_x.reshape(x_in.shape), small[:per_in], d_w_q, shard_side[:, :rank].reshape(-1) * inv_dev,
                small[per_in:per_in + per_kv], shard_side[:, rank:rank + rot].reshape(-1) * inv_dev,
                d_w_uk, d_w_uv, d_w_o.reshape(-1) * inv_dev)

    batch_spec = P('dp')
    full_spec = P()
    return jax.shard_map(device_step, mesh=mesh,
                         in_specs=(batch_spec, batch_spec) + (full_spec,) * 8,
                         out_specs=(batch_spec,) * 9, check_vma=False)
```

time: 1720 us -> 921 us (0.54)
  matrix products: 820 us -> 302 us
  waiting for transfers between devices: 613 us -> 140 us
  Pallas kernels: 0 us -> 228 us
  starting transfers between devices: 0.04 us -> 70.2 us
  local copies, waits for them, and re-layouts: 122 us -> 72.1 us
  blocking collectives: 43.4 us -> 0 us
    unnamed x2 -> x0, waiting for transfers between devices: 613 us -> none
    dot_general x25 -> x24, matrix products: 775 us -> 302 us  [contract(): lax.dot_general(operand_a, operand_b, (((dim_a,), (dim_b,)), ((), ())), p...]
    pallas_call x0 -> x6, Pallas kernels: none -> 228 us  [the longest x2 115 us: attention(): pl.pallas_call(functools.partial(attn_body, heads, qk_scale), grid=(n_seq...]
    ppermute x0 -> x65, waiting for transfers between devices: none -> 140 us  [the longest x55 128 us: transfer(): lax.ppermute(value, 'dp', perms[held[2]])]
    add x0 -> x63, other arithmetic: none -> 82.5 us  [the longest x48 63.6 us: exchange(): send = sum((pick(arr, axis, 1 - bit[name]) for arr in addends))]
    ppermute x0 -> x65, starting transfers between devices: none -> 70.2 us  [the longest x55 62.8 us: transfer(): lax.ppermute(value, 'dp', perms[held[2]])]
    convert_element_type x6 -> x2, other arithmetic: 53.5 us -> 3.4 us  [the longest x1 3.4 us: device_step(): lat_norm = (lat_hat * gain_kv).astype(jnp.bfloat16)]
    dot_general x3 -> x0, local copies, waits for them, and re-layouts: 47.9 us -> none  [contract(): jnp.einsum(eq_form, operand_a, operand_b, preferred_element_type=jnp.floa...]
  transfers between devices with their start and end apart: 1 -> 65, of which waited for: 1 -> 18; matrix products, arithmetic and copies ran while one was open for 7% -> 22% of each run, Pallas kernels for 0% -> 16%
where the time goes in v1:
time: 921 us; the launch traced here: 912 us
  matrix products  302 us (33%)
  Pallas kernels  228 us (25%)
  waiting for transfers between devices  140 us (15%)
  other arithmetic  97.3 us (11%)
  local copies, waits for them, and re-layouts  72.1 us (8%)
  starting transfers between devices  70.2 us (8%)
    dot_general x24, matrix products, contract(): lax.dot_general(operand_a, operand_b, (((dim_a,), (dim_b,)), ((), ())), p...  302 us
    ppermute x55, waiting for transfers between devices, transfer(): lax.ppermute(value, 'dp', perms[held[2]])  128 us
    pallas_call x2, Pallas kernels, attention(): pl.pallas_call(functools.partial(attn_body, heads, qk_scale), grid=(n_seq...  115 us
    pallas_call x3, Pallas kernels, tail(): pl.pallas_call(functools.partial(tail_body, len(acts), len(weights)), gri...  92.5 us
    add x48, other arithmetic, exchange(): send = sum((pick(arr, axis, 1 - bit[name]) for arr in addends))  63.6 us
    ppermute x55, starting transfers between devices, transfer(): lax.ppermute(value, 'dp', perms[held[2]])  62.8 us
    pallas_call x1, Pallas kernels, normalize(): pl.pallas_call(norm_body, grid=(tokens // block,), in_specs=[pl.BlockSpec...  19.9 us
    add x14, other arithmetic, result(): sum(addends)  18.9 us
  transfers between devices with their start and end apart: 65, of which 18 were waited for; matrix products, arithmetic and copies ran while one was open for 22% of the time, Pallas kernels for 16%

profile of v1, /device:TPU:0, one launch (start us, length us, event | category | flops | bytes accessed | tf_op | source)
XLA Modules:
  0.0 912.0 jit_solution(14122704410129531293)
XLA Ops:
  1.3 2.9 copy.26
  4.3 19.9 %shard_map.169 = (bf16[3072,2048]{1,0:T(8,128)(2,1)}, bf16[3072,1024]{1,0:T(8,128)(2,1)}, bf16[3072,1024]{1,0:T(8,128)(2,1)}) custom-call(s32[1]{0:T(128)} %bitcast.core_ref, bf16[3072,2048]{1,0:T(8,128)(2,1)} %bitcast.734, f32[1,2048]{1,0:T(1,128)S(1)} %bitcast.730), custom_call_target="tpu_custom_call" | custom-call | flops 50331648 | bytes 37748736 | tf_op jit(solution)/shard_map/pallas_call | solution.py:58
  24.2 12.6 %fusion.8 = f32[3072,640]{1,0:T(8,128)S(1)} fusion(bf16[3072,2048]{1,0:T(8,128)(2,1)} %get-tuple-element.339, bf16[2048,64]{0,1:T(8,128)(2,1)S(1)} %copy-done.78, bf16[2048,512]{0,1:T(8,128)(2,1)S(1)} %copy.26), kind=kOutput, calls=%fused_computation.40 | convolution fusion | flops 8060928000 | bytes 22806528 | tf_op jit(solution)/shard_map/dot_general | solution.py:17
  37.4 5.3 fusion.71
  42.7 5.5 fusion.70
  48.2 3.4 multiply_convert_fusion.1
  56.1 5.5 convolution_convert_fusion.5.v_ref
  61.6 5.5 convolution_convert_fusion.6.kn_ref
  67.1 17.9 %convolution_convert_fusion.7.qn_ref = bf16[3072,1024]{1,0:T(8,128)(2,1)} fusion(bf16[3072,2048]{1,0:T(8,128)(2,1)} %get-tuple-element.339, bf16[2048,1024]{0,1:T(8,128)(2,1)S(1)} %bitcast.757), kind=kOutput, calls=%fused_computation.13 | convolution fusion | flops 12888047616 | bytes 23068672 | tf_op jit(solution)/shard_map/dot_general | solution.py:17
  85.1 11.6 %fusion.83.qr_ref = f32[3072,512]{1,0:T(8,128)} fusion(bf16[3072,2048]{1,0:T(8,128)(2,1)} %get-tuple-element.339, bf16[2048,512]{0,1:T(8,128)(2,1)S(1)} %bitcast.766), kind=kOutput, calls=%fused_computation.282 | convolution fusion | flops 6442450944 | bytes 20971520 | tf_op jit(solution)/shard_map/dot_general | solution.py:17
  96.7 3.6 fusion.72
  100.7 17.0 %convolution_convert_fusion.4.do_ref = bf16[3072,1024]{1,0:T(8,128)(2,1)} fusion(bf16[3072,2048]{1,0:T(8,128)(2,1)S(1)} %bitcast.745, bf16[1024,2048]{1,0:T(8,128)(2,1)} %bitcast.782), kind=kOutput, calls=%fused_computation.10 | convolution fusion | flops 12888047616 | bytes 23068672 | tf_op jit(solution)/shard_map/dot_general | solution.py:17
  118.0 57.6 %shard_map.170 = (bf16[3072,512]{1,0:T(8,128)(2,1)}, bf16[3072,512]{1,0:T(8,128)(2,1)}, bf16[3072,1536]{1,0:T(8,128)(2,1)}, bf16[3072,2048]{1,0:T(8,128)(2,1)}, f32[3072,128]{1,0:T(8,128)S(1)}) custom-call(s32[1]{0:T(128)} %bitcast.core_ref, bf16[3072,1024]{1,0:T(8,128)(2,1)} %convolution_convert_fusion.7.qn_ref, f32[3072,512]{1,0:T(8,128)} %fusion.83.qr_ref, ...), custom_call_target="tpu_custom_call" | custom-call | flops 10871635968 | bytes 62914560 | tf_op jit(solution)/shard_map/pallas_call | solution.py:127
  175.6 15.7 %fusion.84 = f32[1024,1536]{1,0:T(8,128)} fusion(bf16[3072,1024]{1,0:T(8,128)(2,1)} %get-tuple-element.293, bf16[3072,1536]{1,0:T(8,128)(2,1)} %get-tuple-element.380.refs_0_), kind=kOutput, calls=%fused_computation.283 | convolution fusion | flops 9663676416 | bytes 22020096 | tf_op jit(solution)/shard_map/dot_general | solution.py:17
  191.8 10.7 %fusion.86 = f32[512,2048]{1,0:T(8,128)S(1)} fusion(bf16[3072,512]{1,0:T(8,128)(2,1)} %copy-done.41, bf16[3072,2048]{1,0:T(8,128)(2,1)} %get-tuple-element.323), kind=kOutput, calls=%fused_computation.285 | convolution fusion | flops 6442450944 | bytes 19922944 | tf_op jit(solution)/shard_map/dot_general | solution.py:17
  202.6 11.0 %fusion.85 = f32[512,2048]{1,0:T(8,128)} fusion(bf16[3072,512]{1,0:T(8,128)(2,1)S(1)} %copy-done.115, bf16[3072,2048]{1,0:T(8,128)(2,1)} %bitcast.738), kind=kOutput, calls=%fused_computation.284 | convolution fusion | flops 6442450944 | bytes 19922944 | tf_op jit(solution)/shard_map/dot_general | solution.py:17
  213.6 2.2 dynamic-slice_bitcast_fusion.4
  218.0 15.5 %convolution_add_fusion.2 = f32[1024,1536]{1,0:T(8,128)S(1)} fusion(f32[1024,1536]{1,0:T(8,128)} %collective-permute-done, bf16[3072,1024]{1,0:T(8,128)(2,1)} %get-tuple-element.310, bf16[3072,1536]{1,0:T(8,128)(2,1)} %get-tuple-element.380.refs_0_), kind=kOutput, calls=%fused_computation.16 | convolution fusion | flops 9665249280 | bytes 28311552 | tf_op jit(solution)/shard_map/dot_general | solution.py:17
  240.5 12.0 %fusion.87.qr_ref = f32[3072,512]{1,0:T(8,128)} fusion(bf16[3072,2048]{1,0:T(8,128)(2,1)} %get-tuple-element.339, bf16[2048,512]{0,1:T(8,128)(2,1)S(1)} %bitcast.765), kind=kOutput, calls=%fused_computation.286 | convolution fusion | flops 6442450944 | bytes 20971520 | tf_op jit(solution)/shard_map/dot_general | solution.py:17
  252.5 17.3 %convolution_convert_fusion.3.qn_ref = bf16[3072,1024]{1,0:T(8,128)(2,1)} fusion(bf16[3072,2048]{1,0:T(8,128)(2,1)} %get-tuple-element.339, bf16[2048,1024]{0,1:T(8,128)(2,1)S(1)} %bitcast.756), kind=kOutput, calls=%fused_computation.9 | convolution fusion | flops 12888047616 | bytes 23068672 | tf_op jit(solution)/shard_map/dot_general | solution.py:17
  269.9 2.5 collective-permute-start.5
  274.4 10.3 %convolution_add_fusion.4 = f32[512,2048]{1,0:T(8,128)} fusion(f32[512,2048]{1,0:T(8,128)} %collective-permute-done.1, bf16[3072,512]{1,0:T(8,128)(2,1)} %get-tuple-element.234, bf16[3072,2048]{1,0:T(8,128)(2,1)S(1)} %bitcast.748), kind=kOutput, calls=%fused_computation.19 | convolution fusion | flops 6443499520 | bytes 24117248 | tf_op jit(solution)/shard_map/dot_general | solution.py:17
  284.8 33.9 %collective-permute-done.3 = f32[2,2,2,16,1024]{4,3,2,1,0:T(8,128)S(1)} collective-permute-done((f32[2,2,2,16,1024]{4,3,2,1,0:T(8,128)}, f32[2,2,2,16,1024]{4,3,2,1,0:T(8,128)S(1)}, u32[]{:S(2)}, u32[]{:S(2)}) %collective-permute-start.3) | collective-permute-done | bytes 524320 | tf_op jit(solution)/shard_map/ppermute | solution.py:218
  320.1 3.9 fusion.76
  329.4 2.1 bitcast_add_fusion.3
  338.9 17.1 %convolution_convert_fusion.do_ref = bf16[3072,1024]{1,0:T(8,128)(2,1)} fusion(bf16[3072,2048]{1,0:T(8,128)(2,1)S(1)} %bitcast.749, bf16[1024,2048]{1,0:T(8,128)(2,1)} %bitcast.781), kind=kOutput, calls=%fused_computation.6 | convolution fusion | flops 12888047616 | bytes 23068672 | tf_op jit(solution)/shard_map/dot_general | solution.py:17
  356.0 7.5 convolution_convert_fusion.1.v_ref
  363.5 17.2 %collective-permute-done.7 = f32[2,2,16,1024]{3,2,1,0:T(8,128)} collective-permute-done((f32[2,2,16,1024]{3,2,1,0:T(8,128)}, f32[2,2,16,1024]{3,2,1,0:T(8,128)}, u32[]{:S(2)}, u32[]{:S(2)}) %collective-permute-start.7) | collective-permute-done | bytes 262176 | tf_op jit(solution)/shard_map/ppermute | solution.py:218
  382.0 5.4 convolution_convert_fusion.2.kn_ref
  393.4 2.1 bitcast_add_fusion.15
  406.1 57.7 %shard_map.171 = (bf16[3072,512]{1,0:T(8,128)(2,1)}, bf16[3072,512]{1,0:T(8,128)(2,1)}, bf16[3072,1536]{1,0:T(8,128)(2,1)}, bf16[3072,2048]{1,0:T(8,128)(2,1)}, f32[3072,128]{1,0:T(8,128)S(1)}) custom-call(s32[1]{0:T(128)} %bitcast.core_ref, bf16[3072,1024]{1,0:T(8,128)(2,1)} %convolution_convert_fusion.3.qn_ref, f32[3072,512]{1,0:T(8,128)} %fusion.87.qr_ref, ...), custom_call_target="tpu_custom_call" | custom-call | flops 10871635968 | bytes 62914560 | tf_op jit(solution)/shard_map/pallas_call | solution.py:127
  470.9 2.7 collective-permute-start.19
  475.9 2.6 collective-permute-start.22
  479.4 15.6 %fusion.88 = f32[1024,1536]{1,0:T(8,128)} fusion(bf16[3072,1024]{1,0:T(8,128)(2,1)} %get-tuple-element.293, bf16[3072,1536]{1,0:T(8,128)(2,1)} %get-tuple-element.381.refs_1_), kind=kOutput, calls=%fused_computation.287 | convolution fusion | flops 9663676416 | bytes 22020096 | tf_op jit(solution)/shard_map/dot_general | solution.py:17
  496.7 9.7 %fusion.90 = f32[512,2048]{1,0:T(8,128)S(1)} fusion(bf16[3072,512]{1,0:T(8,128)(2,1)S(1)} %copy-done.43, bf16[3072,2048]{1,0:T(8,128)(2,1)} %get-tuple-element.324), kind=kOutput, calls=%fused_computation.289 | convolution fusion | flops 6442450944 | bytes 19922944 | tf_op jit(solution)/shard_map/dot_general | solution.py:17
  506.4 10.1 %fusion.89 = f32[512,2048]{1,0:T(8,128)} fusion(bf16[3072,512]{1,0:T(8,128)(2,1)} %get-tuple-element.302, bf16[3072,2048]{1,0:T(8,128)(2,1)S(1)} %bitcast.752), kind=kOutput, calls=%fused_computation.288 | convolution fusion | flops 6442450944 | bytes 19922944 | tf_op jit(solution)/shard_map/dot_general | solution.py:17
  516.5 2.5 dynamic-slice_bitcast_fusion.2
  521.0 3.6 fusion.7.refs_7_
  525.2 2.0 copy_bitcast_fusion
  527.4 15.5 %convolution_add_fusion.1 = f32[1024,1536]{1,0:T(8,128)S(1)} fusion(f32[1024,1536]{1,0:T(8,128)} %copy-done.114, bf16[3072,1024]{1,0:T(8,128)(2,1)} %get-tuple-element.310, bf16[3072,1536]{1,0:T(8,128)(2,1)} %get-tuple-element.381.refs_1_), kind=kOutput, calls=%fused_computation.15 | convolution fusion | flops 9665249280 | bytes 28311552 | tf_op jit(solution)/shard_map/dot_general | solution.py:17
  547.5 12.5 %fusion = f32[3072,512]{1,0:T(8,128)} fusion(bf16[3072,2048]{1,0:T(8,128)(2,1)} %get-tuple-element.323, bf16[512,1024]{1,0:T(8,128)(2,1)S(1)} %get-tuple-element.455, bf16[512,1024]{1,0:T(8,128)(2,1)S(1)} %get-tuple-element.456), kind=kOutput, calls=%fused_computation.23 | convolution fusion | flops 6446645248 | bytes 20971520 | tf_op jit(solution)/shard_map/dot_general | solution.py:17
  560.0 16.3 %multiply_reduce_fusion = (f32[3072]{0:T(1024)S(1)}, f32[512]{0:T(512)S(1)}, f32[3072,512]{1,0:T(8,128)}) fusion(f32[3072,512]{1,0:T(8,128)S(1)} %bitcast.771, f32[512]{0:T(512)S(1)} %copy-done.109, f32[3072,512]{1,0:T(8,128)} %fusion, bf16[3072,2048]{1,0:T(8,128)(2,1)} %get-tuple-element.324, bf16[512,1024]{1,0:T(8,128)(2,1)} %get-tuple-element.457, ...), kind=kOutput, calls=%fused_computation.1 | convolution fusion | flops 6456078848 | bytes 33570816 | tf_op jit(solution)/shard_map/dot_general | solution.py:17
  580.4 14.0 %convolution_add_fusion.3 = f32[512,2048]{1,0:T(8,128)} fusion(f32[512,2048]{1,0:T(8,128)} %collective-permute-done.26, bf16[3072,512]{1,0:T(8,128)(2,1)} %get-tuple-element.320, bf16[3072,2048]{1,0:T(8,128)(2,1)} %bitcast.739), kind=kOutput, calls=%fused_computation.18 | convolution fusion | flops 6443499520 | bytes 24117248 | tf_op jit(solution)/shard_map/dot_general | solution.py:17
  594.4 2.1 multiply_convert_fusion
  597.1 27.2 %collective-permute-done.28 = f32[2,2,2,16,1024]{4,3,2,1,0:T(8,128)S(1)} collective-permute-done((f32[2,2,2,16,1024]{4,3,2,1,0:T(8,128)}, f32[2,2,2,16,1024]{4,3,2,1,0:T(8,128)S(1)}, u32[]{:S(2)}, u32[]{:S(2)}) %collective-permute-start.28) | collective-permute-done | bytes 524320 | tf_op jit(solution)/shard_map/ppermute | solution.py:218
  638.6 15.1 %fusion.91 = f32[2048,640]{1,0:T(8,128)} fusion(bf16[3072,2048]{1,0:T(8,128)(2,1)} %get-tuple-element.339, bf16[3072,640]{1,0:T(8,128)(2,1)S(1)} %pad_maximum_fusion.refs_2_), kind=kOutput, calls=%fused_computation.290 | convolution fusion | flops 8053063680 | bytes 21757952 | tf_op jit(solution)/shard_map/dot_general | solution.py:17
  653.7 27.0 %collective-permute-done.32 = f32[2,2,16,1024]{3,2,1,0:T(8,128)S(1)} collective-permute-done((f32[2,2,16,1024]{3,2,1,0:T(8,128)S(1)}, f32[2,2,16,1024]{3,2,1,0:T(8,128)S(1)}, u32[]{:S(2)}, u32[]{:S(2)}) %collective-permute-start.32) | collective-permute-done | bytes 262176 | tf_op jit(solution)/shard_map/ppermute | solution.py:218
  681.8 30.7 %shard_map.172 = (bf16[3072,2048]{1,0:T(8,128)(2,1)}, f32[1,2048]{1,0:T(1,128)}) custom-call(bf16[3072,1536]{1,0:T(8,128)(2,1)} %get-tuple-element.380.refs_0_, bf16[3072,1536]{1,0:T(8,128)(2,1)} %get-tuple-element.381.refs_1_, bf16[3072,640]{1,0:T(8,128)(2,1)} %copy-done.5, bf16[1024,2048]{1,0:T(8,128)(2,1)} %bitcast.758, bf16[512,2048]{1,0:T(8,128)(2,1)} %bitcast.767, ...), custom_call_target="tpu_custom_call" | custom-call | flops 15569256448 | bytes 35389440 | tf_op jit(solution)/shard_map/pallas_call | solution.py:177
  713.9 4.7 dynamic-slice_bitcast_fusion
  718.7 2.0 bitcast_add_fusion.4
  722.7 2.1 bitcast_add_fusion.9
  747.3 30.9 %shard_map.173 = (bf16[3072,2048]{1,0:T(8,128)(2,1)}, f32[1,2048]{1,0:T(1,128)}) custom-call(bf16[3072,1536]{1,0:T(8,128)(2,1)} %get-tuple-element.380.refs_0_, bf16[3072,1536]{1,0:T(8,128)(2,1)} %get-tuple-element.381.refs_1_, bf16[3072,640]{1,0:T(8,128)(2,1)} %copy-done.5, bf16[1024,2048]{1,0:T(8,128)(2,1)} %bitcast.759, ...), custom_call_target="tpu_custom_call", output_to_operand_aliasing={{0}: (11, {})} | custom-call | flops 15569256448 | bytes 35389440 | tf_op jit(solution)/shard_map/pallas_call | solution.py:177
  778.5 2.3 slice.165
  782.8 2.3 bitcast_add_fusion.26
  798.1 2.2 collective-permute-start.45
  805.2 5.5 collective-permute-done.45
  814.6 30.9 %shard_map.174 = (bf16[3072,2048]{1,0:T(8,128)(2,1)}, f32[1,2048]{1,0:T(1,128)}) custom-call(bf16[3072,1536]{1,0:T(8,128)(2,1)} %get-tuple-element.380.refs_0_, bf16[3072,1536]{1,0:T(8,128)(2,1)} %get-tuple-element.381.refs_1_, bf16[3072,640]{1,0:T(8,128)(2,1)} %copy-done.5, bf16[1024,2048]{1,0:T(8,128)(2,1)} %bitcast.760, ...), custom_call_target="tpu_custom_call", output_to_operand_aliasing={{0}: (11, {})} | custom-call | flops 15569256448 | bytes 35389440 | tf_op jit(solution)/shard_map/pallas_call | solution.py:177
  858.1 2.1 bitcast_add_fusion.8
  863.5 8.2 collective-permute-done.54
  877.0 2.0 collective-permute-done.56
  887.2 3.1 collective-permute-done.59
  891.2 2.4 collective-permute-start.60
  897.4 4.1 collective-permute-done.62
  905.4 3.6 collective-permute-done.63
  (497 shorter events, 179.0 us)
Async XLA Ops:
  191.3 22.3 %collective-permute-start = (f32[1024,1536]{1,0:T(8,128)}, f32[1024,1536]{1,0:T(8,128)}, u32[]{:S(2)}, u32[]{:S(2)}) collective-permute-start(f32[1024,1536]{1,0:T(8,128)} %fusion.84), channel_id=1, source_target_pairs={{0,1},{1,0},{2,3},{3,2},{4,5},{5,4},{6,7},{7,6},{8,9},{9,8},{10,11... | collective-permute-start | bytes 18874376 | tf_op jit(solution)/shard_map/ppermute | solution.py:254
  215.8 17.8 %collective-permute-start.1 = (f32[512,2048]{1,0:T(8,128)}, f32[512,2048]{1,0:T(8,128)}, u32[]{:S(2)}, u32[]{:S(2)}) collective-permute-start(f32[512,2048]{1,0:T(8,128)} %fusion.85), channel_id=1, source_target_pairs={{0,1},{1,0},{2,3},{3,2},{4,5},{5,4},{6,7},{7,6},{8,9},{9,8},{10,11... | collective-permute-start | bytes 12582920 | tf_op jit(solution)/shard_map/ppermute | solution.py:254
  215.8 17.7 %collective-permute-start.2 = (f32[2,2,2,2,16,2048]{5,4,3,2,1,0:T(8,128)}, f32[2,2,2,2,16,2048]{5,4,3,2,1,0:T(8,128)S(1)}, u32[]{:S(2)}, u32[]{:S(2)}) collective-permute-start(f32[2,2,2,2,16,2048]{5,4,3,2,1,0:T(8,128)} %get-tuple-element.230), channel_id=1, source_target_pairs={{0,1},{1,0},{2,3},{3,2},{4,5},{5,4},{6,7},{7,6},{8,9},{9,8},{10,11... | collective-permute-start | bytes 6291464 | tf_op jit(solution)/shard_map/ppermute | solution.py:218
  269.9 50.3 %collective-permute-start.5 = (f32[2,2,2,64,768]{4,3,2,1,0:T(8,128)}, f32[2,2,2,64,768]{4,3,2,1,0:T(8,128)S(1)}, u32[]{:S(2)}, u32[]{:S(2)}) collective-permute-start(f32[2,2,2,64,768]{4,3,2,1,0:T(8,128)} %dynamic-slice_bitcast_fusion.9), channel_id=1, source_target_pairs={{0,2},{1,3},{2,0},{3,1},{4,6},{5,7},{6,4},{7,5},{8,10},{9,11},{10,... | collective-permute-start | bytes 4718600 | tf_op jit(solution)/shard_map/ppermute | solution.py:218
  272.3 47.8 %collective-permute-start.6 = (f32[2,2,2,64,768]{4,3,2,1,0:T(8,128)S(1)}, f32[2,2,2,64,768]{4,3,2,1,0:T(8,128)S(1)}, u32[]{:S(2)}, u32[]{:S(2)}) collective-permute-start(f32[2,2,2,64,768]{4,3,2,1,0:T(8,128)S(1)} %copy-done.57), channel_id=1, source_target_pairs={{0,4},{1,5},{2,6},{3,7},{4,0},{5,1},{6,2},{7,3},{8,12},{9,13},{10,... | collective-permute-start | bytes 4718600 | tf_op jit(solution)/shard_map/ppermute | solution.py:218
  273.9 44.8 %collective-permute-start.3 = (f32[2,2,2,16,1024]{4,3,2,1,0:T(8,128)}, f32[2,2,2,16,1024]{4,3,2,1,0:T(8,128)S(1)}, u32[]{:S(2)}, u32[]{:S(2)}) collective-permute-start(f32[2,2,2,16,1024]{4,3,2,1,0:T(8,128)} %add_bitcast_fusion.5), channel_id=1, source_target_pairs={{0,2},{1,3},{2,0},{3,1},{4,6},{5,7},{6,4},{7,5},{8,10},{9,11},{10,... | collective-permute-start | bytes 1572872 | tf_op jit(solution)/shard_map/ppermute | solution.py:218
  274.4 45.7 %collective-permute-start.4 = (f32[2,2,2,16,1024]{4,3,2,1,0:T(8,128)S(1)}, f32[2,2,2,16,1024]{4,3,2,1,0:T(8,128)S(1)}, u32[]{:S(2)}, u32[]{:S(2)}) collective-permute-start(f32[2,2,2,16,1024]{4,3,2,1,0:T(8,128)S(1)} %copy-done.73), channel_id=1, source_target_pairs={{0,4},{1,5},{2,6},{3,7},{4,0},{5,1},{6,2},{7,3},{8,12},{9,13},{10,... | collective-permute-start | bytes 1572872 | tf_op jit(solution)/shard_map/ppermute | solution.py:218
  333.3 54.2 %collective-permute-start.11 = (f32[2,2,64,1024]{3,2,1,0:T(8,128)}, f32[2,2,64,1024]{3,2,1,0:T(8,128)}, u32[]{:S(2)}, u32[]{:S(2)}) collective-permute-start(f32[2,2,64,1024]{3,2,1,0:T(8,128)} %dynamic-slice_bitcast_fusion.13), channel_id=1, source_target_pairs={{0,2},{1,3},{2,0},{3,1},{4,6},{5,7},{6,4},{7,5},{8,10},{9,11},{10,... | collective-permute-start | bytes 3145736 | tf_op jit(solution)/shard_map/ppermute | solution.py:218
  333.8 53.8 %collective-permute-start.12 = (f32[2,2,64,1024]{3,2,1,0:T(8,128)}, f32[2,2,64,1024]{3,2,1,0:T(8,128)}, u32[]{:S(2)}, u32[]{:S(2)}) collective-permute-start(f32[2,2,64,1024]{3,2,1,0:T(8,128)} %dynamic-slice_bitcast_fusion.12), channel_id=1, source_target_pairs={{0,4},{1,5},{2,6},{3,7},{4,0},{5,1},{6,2},{7,3},{8,12},{9,13},{10,... | collective-permute-start | bytes 3145736 | tf_op jit(solution)/shard_map/ppermute | solution.py:218
  335.4 52.2 %collective-permute-start.10 = (f32[2,2,64,768]{3,2,1,0:T(8,128)}, f32[2,2,64,768]{3,2,1,0:T(8,128)}, u32[]{:S(2)}, u32[]{:S(2)}) collective-permute-start(f32[2,2,64,768]{3,2,1,0:T(8,128)} %bitcast_add_fusion.2), channel_id=1, source_target_pairs={{0,2},{1,3},{2,0},{3,1},{4,6},{5,7},{6,4},{7,5},{8,10},{9,11},{10,... | collective-permute-start | bytes 2359304 | tf_op jit(solution)/shard_map/ppermute | solution.py:218
  336.9 50.7 %collective-permute-start.9 = (f32[2,2,64,768]{3,2,1,0:T(8,128)}, f32[2,2,64,768]{3,2,1,0:T(8,128)}, u32[]{:S(2)}, u32[]{:S(2)}) collective-permute-start(f32[2,2,64,768]{3,2,1,0:T(8,128)} %bitcast_add_fusion.3), channel_id=1, source_target_pairs={{0,4},{1,5},{2,6},{3,7},{4,0},{5,1},{6,2},{7,3},{8,12},{9,13},{10,... | collective-permute-start | bytes 2359304 | tf_op jit(solution)/shard_map/ppermute | solution.py:218
  337.4 43.3 %collective-permute-start.7 = (f32[2,2,16,1024]{3,2,1,0:T(8,128)}, f32[2,2,16,1024]{3,2,1,0:T(8,128)}, u32[]{:S(2)}, u32[]{:S(2)}) collective-permute-start(f32[2,2,16,1024]{3,2,1,0:T(8,128)} %bitcast_add_fusion.37), channel_id=1, source_target_pairs={{0,4},{1,5},{2,6},{3,7},{4,0},{5,1},{6,2},{7,3},{8,12},{9,13},{10,... | collective-permute-start | bytes 786440 | tf_op jit(solution)/shard_map/ppermute | solution.py:218
  380.7 6.8 collective-permute-start.8
  398.3 6.2 collective-permute-start.13
  399.8 64.1 %collective-permute-start.17 = (f32[2,64,1024]{2,1,0:T(8,128)}, f32[2,64,1024]{2,1,0:T(8,128)S(1)}, u32[]{:S(2)}, u32[]{:S(2)}) collective-permute-start(f32[2,64,1024]{2,1,0:T(8,128)} %bitcast_add_fusion.7), channel_id=1, source_target_pairs={{0,4},{1,5},{2,6},{3,7},{4,0},{5,1},{6,2},{7,3},{8,12},{9,13},{10,... | collective-permute-start | bytes 1572872 | tf_op jit(solution)/shard_map/ppermute | solution.py:218
  401.3 62.6 %collective-permute-start.18 = (f32[2,64,1024]{2,1,0:T(8,128)}, f32[2,64,1024]{2,1,0:T(8,128)S(1)}, u32[]{:S(2)}, u32[]{:S(2)}) collective-permute-start(f32[2,64,1024]{2,1,0:T(8,128)} %bitcast_add_fusion.6), channel_id=1, source_target_pairs={{0,2},{1,3},{2,0},{3,1},{4,6},{5,7},{6,4},{7,5},{8,10},{9,11},{10,... | collective-permute-start | bytes 1572872 | tf_op jit(solution)/shard_map/ppermute | solution.py:218
  402.4 61.5 %collective-permute-start.15 = (f32[2,64,768]{2,1,0:T(8,128)}, f32[2,64,768]{2,1,0:T(8,128)S(1)}, u32[]{:S(2)}, u32[]{:S(2)}) collective-permute-start(f32[2,64,768]{2,1,0:T(8,128)} %bitcast_add_fusion.15), channel_id=1, source_target_pairs={{0,8},{1,9},{2,10},{3,11},{4,12},{5,13},{6,14},{7,15},{8,0},{9,1},... | collective-permute-start | bytes 1179656 | tf_op jit(solution)/shard_map/ppermute | solution.py:218
  402.8 61.0 %collective-permute-start.16 = (f32[2,64,768]{2,1,0:T(8,128)}, f32[2,64,768]{2,1,0:T(8,128)S(1)}, u32[]{:S(2)}, u32[]{:S(2)}) collective-permute-start(f32[2,64,768]{2,1,0:T(8,128)} %bitcast_add_fusion.13), channel_id=1, source_target_pairs={{0,8},{1,9},{2,10},{3,11},{4,12},{5,13},{6,14},{7,15},{8,0},{9,1},... | collective-permute-start | bytes 1179656 | tf_op jit(solution)/shard_map/ppermute | solution.py:218
  404.5 59.4 %collective-permute-start.14 = (f32[2,16,1024]{2,1,0:T(8,128)S(1)}, f32[2,16,1024]{2,1,0:T(8,128)S(1)}, u32[]{:S(2)}, u32[]{:S(2)}) collective-permute-start(f32[2,16,1024]{2,1,0:T(8,128)S(1)} %bitcast_add_fusion.70), channel_id=1, source_target_pairs={{0,8},{1,9},{2,10},{3,11},{4,12},{5,13},{6,14},{7,15},{8,0},{9,1},... | collective-permute-start | bytes 393224 | tf_op jit(solution)/shard_map/ppermute | solution.py:218
  470.9 7.6 collective-permute-start.19
  473.6 21.6 %collective-permute-start.23 = (f32[64,1024]{1,0:T(8,128)S(1)}, f32[64,1024]{1,0:T(8,128)S(1)}, u32[]{:S(2)}, u32[]{:S(2)}) collective-permute-start(f32[64,1024]{1,0:T(8,128)S(1)} %bitcast_add_fusion.34), channel_id=1, source_target_pairs={{0,8},{1,9},{2,10},{3,11},{4,12},{5,13},{6,14},{7,15},{8,0},{9,1},... | collective-permute-start | bytes 786440 | tf_op jit(solution)/shard_map/ppermute | solution.py:218
  473.8 21.3 %collective-permute-start.24 = (f32[64,1024]{1,0:T(8,128)S(1)}, f32[64,1024]{1,0:T(8,128)S(1)}, u32[]{:S(2)}, u32[]{:S(2)}) collective-permute-start(f32[64,1024]{1,0:T(8,128)S(1)} %bitcast_add_fusion.32), channel_id=1, source_target_pairs={{0,8},{1,9},{2,10},{3,11},{4,12},{5,13},{6,14},{7,15},{8,0},{9,1},... | collective-permute-start | bytes 786440 | tf_op jit(solution)/shard_map/ppermute | solution.py:218
  475.6 19.5 %collective-permute-start.21 = (f32[64,768]{1,0:T(8,128)S(1)}, f32[64,768]{1,0:T(8,128)S(1)}, u32[]{:S(2)}, u32[]{:S(2)}) collective-permute-start(f32[64,768]{1,0:T(8,128)S(1)} %bitcast_add_fusion.61), channel_id=1, source_target_pairs={{0,16},{1,17},{2,18},{3,19},{4,20},{5,21},{6,22},{7,23},{8,24},{9,... | collective-permute-start | bytes 589832 | tf_op jit(solution)/shard_map/ppermute | solution.py:218
  475.9 19.2 %collective-permute-start.22 = (f32[64,768]{1,0:T(8,128)S(1)}, f32[64,768]{1,0:T(8,128)S(1)}, u32[]{:S(2)}, u32[]{:S(2)}) collective-permute-start(f32[64,768]{1,0:T(8,128)S(1)} %bitcast_add_fusion.58), channel_id=1, source_target_pairs={{0,16},{1,17},{2,18},{3,19},{4,20},{5,21},{6,22},{7,23},{8,24},{9,... | collective-permute-start | bytes 589832 | tf_op jit(solution)/shard_map/ppermute | solution.py:218
  478.5 16.6 %collective-permute-start.20 = (f32[16,1024]{1,0:T(8,128)S(1)}, f32[16,1024]{1,0:T(8,128)S(1)}, u32[]{:S(2)}, u32[]{:S(2)}) collective-permute-start(f32[16,1024]{1,0:T(8,128)S(1)} %bitcast_add_fusion.104), channel_id=1, source_target_pairs={{0,16},{1,17},{2,18},{3,19},{4,20},{5,21},{6,22},{7,23},{8,24},{9,... | collective-permute-start | bytes 196616 | tf_op jit(solution)/shard_map/ppermute | solution.py:218
  496.7 19.8 %collective-permute-start.25 = (f32[1024,1536]{1,0:T(8,128)}, f32[1024,1536]{1,0:T(8,128)S(1)}, u32[]{:S(2)}, u32[]{:S(2)}) collective-permute-start(f32[1024,1536]{1,0:T(8,128)} %fusion.88), channel_id=1, source_target_pairs={{0,1},{1,0},{2,3},{3,2},{4,5},{5,4},{6,7},{7,6},{8,9},{9,8},{10,11... | collective-permute-start | bytes 18874376 | tf_op jit(solution)/shard_map/ppermute | solution.py:254
  520.4 22.5 %collective-permute-start.26 = (f32[512,2048]{1,0:T(8,128)}, f32[512,2048]{1,0:T(8,128)}, u32[]{:S(2)}, u32[]{:S(2)}) collective-permute-start(f32[512,2048]{1,0:T(8,128)} %fusion.89), channel_id=1, source_target_pairs={{0,1},{1,0},{2,3},{3,2},{4,5},{5,4},{6,7},{7,6},{8,9},{9,8},{10,11... | collective-permute-start | bytes 12582920 | tf_op jit(solution)/shard_map/ppermute | solution.py:254
  527.2 15.8 %collective-permute-start.27 = (f32[2,2,2,2,16,2048]{5,4,3,2,1,0:T(8,128)S(1)}, f32[2,2,2,2,16,2048]{5,4,3,2,1,0:T(8,128)S(1)}, u32[]{:S(2)}, u32[]{:S(2)}) collective-permute-start(f32[2,2,2,2,16,2048]{5,4,3,2,1,0:T(8,128)S(1)} %copy-done.50), channel_id=1, source_target_pairs={{0,1},{1,0},{2,3},{3,2},{4,5},{5,4},{6,7},{7,6},{8,9},{9,8},{10,11... | collective-permute-start | bytes 6291464 | tf_op jit(solution)/shard_map/ppermute | solution.py:218
  576.2 48.9 %collective-permute-start.30 = (f32[2,2,2,64,768]{4,3,2,1,0:T(8,128)}, f32[2,2,2,64,768]{4,3,2,1,0:T(8,128)S(1)}, u32[]{:S(2)}, u32[]{:S(2)}) collective-permute-start(f32[2,2,2,64,768]{4,3,2,1,0:T(8,128)} %dynamic-slice_bitcast_fusion.7), channel_id=1, source_target_pairs={{0,2},{1,3},{2,0},{3,1},{4,6},{5,7},{6,4},{7,5},{8,10},{9,11},{10,... | collective-permute-start | bytes 4718600 | tf_op jit(solution)/shard_map/ppermute | solution.py:218
  577.4 47.7 %collective-permute-start.31 = (f32[2,2,2,64,768]{4,3,2,1,0:T(8,128)S(1)}, f32[2,2,2,64,768]{4,3,2,1,0:T(8,128)S(1)}, u32[]{:S(2)}, u32[]{:S(2)}) collective-permute-start(f32[2,2,2,64,768]{4,3,2,1,0:T(8,128)S(1)} %dynamic-slice_bitcast_fusion.6), channel_id=1, source_target_pairs={{0,4},{1,5},{2,6},{3,7},{4,0},{5,1},{6,2},{7,3},{8,12},{9,13},{10,... | collective-permute-start | bytes 4718600 | tf_op jit(solution)/shard_map/ppermute | solution.py:218
  578.9 45.4 %collective-permute-start.28 = (f32[2,2,2,16,1024]{4,3,2,1,0:T(8,128)}, f32[2,2,2,16,1024]{4,3,2,1,0:T(8,128)S(1)}, u32[]{:S(2)}, u32[]{:S(2)}) collective-permute-start(f32[2,2,2,16,1024]{4,3,2,1,0:T(8,128)} %add_bitcast_fusion.3), channel_id=1, source_target_pairs={{0,2},{1,3},{2,0},{3,1},{4,6},{5,7},{6,4},{7,5},{8,10},{9,11},{10,... | collective-permute-start | bytes 1572872 | tf_op jit(solution)/shard_map/ppermute | solution.py:218
  579.8 45.3 %collective-permute-start.29 = (f32[2,2,2,16,1024]{4,3,2,1,0:T(8,128)}, f32[2,2,2,16,1024]{4,3,2,1,0:T(8,128)}, u32[]{:S(2)}, u32[]{:S(2)}) collective-permute-start(f32[2,2,2,16,1024]{4,3,2,1,0:T(8,128)} %add_bitcast_fusion.2), channel_id=1, source_target_pairs={{0,4},{1,5},{2,6},{3,7},{4,0},{5,1},{6,2},{7,3},{8,12},{9,13},{10,... | collective-permute-start | bytes 1572872 | tf_op jit(solution)/shard_map/ppermute | solution.py:218
  633.0 79.5 %collective-permute-start.36 = (f32[2,2,64,1024]{3,2,1,0:T(8,128)}, f32[2,2,64,1024]{3,2,1,0:T(8,128)S(1)}, u32[]{:S(2)}, u32[]{:S(2)}) collective-permute-start(f32[2,2,64,1024]{3,2,1,0:T(8,128)} %dynamic-slice_bitcast_fusion.11), channel_id=1, source_target_pairs={{0,2},{1,3},{2,0},{3,1},{4,6},{5,7},{6,4},{7,5},{8,10},{9,11},{10,... | collective-permute-start | bytes 3145736 | tf_op jit(solution)/shard_map/ppermute | solution.py:218
  634.0 78.5 %collective-permute-start.37 = (f32[2,2,64,1024]{3,2,1,0:T(8,128)}, f32[2,2,64,1024]{3,2,1,0:T(8,128)S(1)}, u32[]{:S(2)}, u32[]{:S(2)}) collective-permute-start(f32[2,2,64,1024]{3,2,1,0:T(8,128)} %dynamic-slice_bitcast_fusion.10), channel_id=1, source_target_pairs={{0,4},{1,5},{2,6},{3,7},{4,0},{5,1},{6,2},{7,3},{8,12},{9,13},{10,... | collective-permute-start | bytes 3145736 | tf_op jit(solution)/shard_map/ppermute | solution.py:218
  635.5 77.0 %collective-permute-start.34 = (f32[2,2,64,768]{3,2,1,0:T(8,128)}, f32[2,2,64,768]{3,2,1,0:T(8,128)}, u32[]{:S(2)}, u32[]{:S(2)}) collective-permute-start(f32[2,2,64,768]{3,2,1,0:T(8,128)} %bitcast_add_fusion.1), channel_id=1, source_target_pairs={{0,4},{1,5},{2,6},{3,7},{4,0},{5,1},{6,2},{7,3},{8,12},{9,13},{10,... | collective-permute-start | bytes 2359304 | tf_op jit(solution)/shard_map/ppermute | solution.py:218
  636.0 76.5 %collective-permute-start.35 = (f32[2,2,64,768]{3,2,1,0:T(8,128)}, f32[2,2,64,768]{3,2,1,0:T(8,128)}, u32[]{:S(2)}, u32[]{:S(2)}) collective-permute-start(f32[2,2,64,768]{3,2,1,0:T(8,128)} %bitcast_add_fusion), channel_id=1, source_target_pairs={{0,2},{1,3},{2,0},{3,1},{4,6},{5,7},{6,4},{7,5},{8,10},{9,11},{10,... | collective-permute-start | bytes 2359304 | tf_op jit(solution)/shard_map/ppermute | solution.py:218
  637.2 43.5 %collective-permute-start.32 = (f32[2,2,16,1024]{3,2,1,0:T(8,128)S(1)}, f32[2,2,16,1024]{3,2,1,0:T(8,128)S(1)}, u32[]{:S(2)}, u32[]{:S(2)}) collective-permute-start(f32[2,2,16,1024]{3,2,1,0:T(8,128)S(1)} %bitcast_add_fusion.31), channel_id=1, source_target_pairs={{0,4},{1,5},{2,6},{3,7},{4,0},{5,1},{6,2},{7,3},{8,12},{9,13},{10,... | collective-permute-start | bytes 786440 | tf_op jit(solution)/shard_map/ppermute | solution.py:218
  680.7 31.8 %collective-permute-start.33 = (f32[2,2,16,1024]{3,2,1,0:T(8,128)S(1)}, f32[2,2,16,1024]{3,2,1,0:T(8,128)S(1)}, u32[]{:S(2)}, u32[]{:S(2)}) collective-permute-start(f32[2,2,16,1024]{3,2,1,0:T(8,128)S(1)} %bitcast_add_fusion.30), channel_id=1, source_target_pairs={{0,2},{1,3},{2,0},{3,1},{4,6},{5,7},{6,4},{7,5},{8,10},{9,11},{10,... | collective-permute-start | bytes 786440 | tf_op jit(solution)/shard_map/ppermute | solution.py:218
  729.0 49.5 %collective-permute-start.44 = (f32[2,2,2,2,64,640]{5,4,3,2,1,0:T(8,128)}, f32[2,2,2,2,64,640]{5,4,3,2,1,0:T(8,128)}, u32[]{:S(2)}, u32[]{:S(2)}) collective-permute-start(f32[2,2,2,2,64,640]{5,4,3,2,1,0:T(8,128)} %get-tuple-element.371), channel_id=1, source_target_pairs={{0,1},{1,0},{2,3},{3,2},{4,5},{5,4},{6,7},{7,6},{8,9},{9,8},{10,11... | collective-permute-start | bytes 7864328 | tf_op jit(solution)/shard_map/ppermute | solution.py:218
  735.8 6.4 collective-permute-start.38
  737.4 7.5 collective-permute-start.39
  739.4 39.1 %collective-permute-start.42 = (f32[2,64,1024]{2,1,0:T(8,128)}, f32[2,64,1024]{2,1,0:T(8,128)}, u32[]{:S(2)}, u32[]{:S(2)}) collective-permute-start(f32[2,64,1024]{2,1,0:T(8,128)} %bitcast_add_fusion.5), channel_id=1, source_target_pairs={{0,4},{1,5},{2,6},{3,7},{4,0},{5,1},{6,2},{7,3},{8,12},{9,13},{10,... | collective-permute-start | bytes 1572872 | tf_op jit(solution)/shard_map/ppermute | solution.py:218
  740.8 37.6 %collective-permute-start.43 = (f32[2,64,1024]{2,1,0:T(8,128)}, f32[2,64,1024]{2,1,0:T(8,128)}, u32[]{:S(2)}, u32[]{:S(2)}) collective-permute-start(f32[2,64,1024]{2,1,0:T(8,128)} %bitcast_add_fusion.4), channel_id=1, source_target_pairs={{0,2},{1,3},{2,0},{3,1},{4,6},{5,7},{6,4},{7,5},{8,10},{9,11},{10,... | collective-permute-start | bytes 1572872 | tf_op jit(solution)/shard_map/ppermute | solution.py:218
  742.1 36.3 %collective-permute-start.40 = (f32[2,64,768]{2,1,0:T(8,128)}, f32[2,64,768]{2,1,0:T(8,128)}, u32[]{:S(2)}, u32[]{:S(2)}) collective-permute-start(f32[2,64,768]{2,1,0:T(8,128)} %bitcast_add_fusion.11), channel_id=1, source_target_pairs={{0,8},{1,9},{2,10},{3,11},{4,12},{5,13},{6,14},{7,15},{8,0},{9,1},... | collective-permute-start | bytes 1179656 | tf_op jit(solution)/shard_map/ppermute | solution.py:218
  745.6 32.8 %collective-permute-start.41 = (f32[2,64,768]{2,1,0:T(8,128)}, f32[2,64,768]{2,1,0:T(8,128)}, u32[]{:S(2)}, u32[]{:S(2)}) collective-permute-start(f32[2,64,768]{2,1,0:T(8,128)} %bitcast_add_fusion.9), channel_id=1, source_target_pairs={{0,8},{1,9},{2,10},{3,11},{4,12},{5,13},{6,14},{7,15},{8,0},{9,1},... | collective-permute-start | bytes 1179656 | tf_op jit(solution)/shard_map/ppermute | solution.py:218
  795.7 17.1 %collective-permute-start.47 = (f32[64,768]{1,0:T(8,128)}, f32[64,768]{1,0:T(8,128)}, u32[]{:S(2)}, u32[]{:S(2)}) collective-permute-start(f32[64,768]{1,0:T(8,128)} %bitcast_add_fusion.55), channel_id=1, source_target_pairs={{0,16},{1,17},{2,18},{3,19},{4,20},{5,21},{6,22},{7,23},{8,24},{9,... | collective-permute-start | bytes 589832 | tf_op jit(solution)/shard_map/ppermute | solution.py:218
  798.1 12.7 %collective-permute-start.45 = (f32[16,1024]{1,0:T(8,128)}, f32[16,1024]{1,0:T(8,128)}, u32[]{:S(2)}, u32[]{:S(2)}) collective-permute-start(f32[16,1024]{1,0:T(8,128)} %bitcast_add_fusion.101), channel_id=1, source_target_pairs={{0,16},{1,17},{2,18},{3,19},{4,20},{5,21},{6,22},{7,23},{8,24},{9,... | collective-permute-start | bytes 196616 | tf_op jit(solution)/shard_map/ppermute | solution.py:218
  800.3 11.9 %collective-permute-start.46 = (f32[16,1024]{1,0:T(8,128)}, f32[16,1024]{1,0:T(8,128)}, u32[]{:S(2)}, u32[]{:S(2)}) collective-permute-start(f32[16,1024]{1,0:T(8,128)} %bitcast_add_fusion.98), channel_id=1, source_target_pairs={{0,16},{1,17},{2,18},{3,19},{4,20},{5,21},{6,22},{7,23},{8,24},{9,... | collective-permute-start | bytes 196616 | tf_op jit(solution)/shard_map/ppermute | solution.py:218
  802.7 43.0 %collective-permute-start.52 = (f32[2,2,2,64,384]{4,3,2,1,0:T(8,128)}, f32[2,2,2,64,384]{4,3,2,1,0:T(8,128)S(1)}, u32[]{:S(2)}, u32[]{:S(2)}) collective-permute-start(f32[2,2,2,64,384]{4,3,2,1,0:T(8,128)} %add_bitcast_fusion), channel_id=1, source_target_pairs={{0,4},{1,5},{2,6},{3,7},{4,0},{5,1},{6,2},{7,3},{8,12},{9,13},{10,... | collective-permute-start | bytes 2359304 | tf_op jit(solution)/shard_map/ppermute | solution.py:218
  804.3 41.4 %collective-permute-start.51 = (f32[2,2,2,64,256]{4,3,2,1,0:T(8,128)}, f32[2,2,2,64,256]{4,3,2,1,0:T(8,128)S(1)}, u32[]{:S(2)}, u32[]{:S(2)}) collective-permute-start(f32[2,2,2,64,256]{4,3,2,1,0:T(8,128)} %add_bitcast_fusion.1), channel_id=1, source_target_pairs={{0,2},{1,3},{2,0},{3,1},{4,6},{5,7},{6,4},{7,5},{8,10},{9,11},{10,... | collective-permute-start | bytes 1572872 | tf_op jit(solution)/shard_map/ppermute | solution.py:218
  810.8 34.9 %collective-permute-start.49 = (f32[64,1024]{1,0:T(8,128)}, f32[64,1024]{1,0:T(8,128)S(1)}, u32[]{:S(2)}, u32[]{:S(2)}) collective-permute-start(f32[64,1024]{1,0:T(8,128)} %bitcast_add_fusion.28), channel_id=1, source_target_pairs={{0,8},{1,9},{2,10},{3,11},{4,12},{5,13},{6,14},{7,15},{8,0},{9,1},... | collective-permute-start | bytes 786440 | tf_op jit(solution)/shard_map/ppermute | solution.py:218
  812.2 33.5 %collective-permute-start.50 = (f32[64,1024]{1,0:T(8,128)}, f32[64,1024]{1,0:T(8,128)S(1)}, u32[]{:S(2)}, u32[]{:S(2)}) collective-permute-start(f32[64,1024]{1,0:T(8,128)} %bitcast_add_fusion.26), channel_id=1, source_target_pairs={{0,8},{1,9},{2,10},{3,11},{4,12},{5,13},{6,14},{7,15},{8,0},{9,1},... | collective-permute-start | bytes 786440 | tf_op jit(solution)/shard_map/ppermute | solution.py:218
  812.8 32.8 %collective-permute-start.48 = (f32[64,768]{1,0:T(8,128)}, f32[64,768]{1,0:T(8,128)S(1)}, u32[]{:S(2)}, u32[]{:S(2)}) collective-permute-start(f32[64,768]{1,0:T(8,128)} %bitcast_add_fusion.52), channel_id=1, source_target_pairs={{0,16},{1,17},{2,18},{3,19},{4,20},{5,21},{6,22},{7,23},{8,24},{9,... | collective-permute-start | bytes 589832 | tf_op jit(solution)/shard_map/ppermute | solution.py:218
  850.0 53.4 %collective-permute-start.64 = (f32[64,2048]{1,0:T(8,128)}, f32[64,2048]{1,0:T(8,128)}, u32[]{:S(2)}, u32[]{:S(2)}) collective-permute-start(f32[64,2048]{1,0:T(8,128)} %fusion.9), channel_id=1, source_target_pairs={{0,16},{1,17},{2,18},{3,19},{4,20},{5,21},{6,22},{7,23},{8,24},{9,... | collective-permute-start | bytes 1572872 | tf_op jit(solution)/shard_map/ppermute | solution.py:378
  856.3 27.8 %collective-permute-start.58 = (f32[2,2,64,256]{3,2,1,0:T(8,128)}, f32[2,2,64,256]{3,2,1,0:T(8,128)}, u32[]{:S(2)}, u32[]{:S(2)}) collective-permute-start(f32[2,2,64,256]{3,2,1,0:T(8,128)} %bitcast_add_fusion.25), channel_id=1, source_target_pairs={{0,4},{1,5},{2,6},{3,7},{4,0},{5,1},{6,2},{7,3},{8,12},{9,13},{10,... | collective-permute-start | bytes 786440 | tf_op jit(solution)/shard_map/ppermute | solution.py:218
  860.2 33.4 %collective-permute-start.61 = (f32[2,2,64,384]{3,2,1,0:T(8,128)}, f32[2,2,64,384]{3,2,1,0:T(8,128)}, u32[]{:S(2)}, u32[]{:S(2)}) collective-permute-start(f32[2,2,64,384]{3,2,1,0:T(8,128)} %bitcast_add_fusion.8), channel_id=1, source_target_pairs={{0,2},{1,3},{2,0},{3,1},{4,6},{5,7},{6,4},{7,5},{8,10},{9,11},{10,... | collective-permute-start | bytes 1179656 | tf_op jit(solution)/shard_map/ppermute | solution.py:218
  861.1 10.7 %collective-permute-start.54 = (f32[2,2,2,1,128]{4,3,2,1,0:T(1,128)S(1)}, f32[2,2,2,1,128]{4,3,2,1,0:T(1,128)S(1)}, u32[]{:S(2)}, u32[]{:S(2)}) collective-permute-start(f32[2,2,2,1,128]{4,3,2,1,0:T(1,128)S(1)} %fusion.35), channel_id=1, source_target_pairs={{0,2},{1,3},{2,0},{3,1},{4,6},{5,7},{6,4},{7,5},{8,10},{9,11},{10,... | collective-permute-start | bytes 12296 | tf_op jit(solution)/shard_map/ppermute | solution.py:373
  871.8 3.6 collective-permute-start.55
  875.4 3.6 collective-permute-start.56
  879.0 4.5 collective-permute-start.57
  885.2 5.0 collective-permute-start.59
  891.2 5.2 collective-permute-start.60
  894.8 6.6 collective-permute-start.62
  902.5 6.5 collective-permute-start.63
  (131 other events, 2022.2 us)
